TPU v7x, 32 devices: a whole 2x2x4 slice. The times are simulated.
32 devices in a mesh: runs: 1, cfg: 32 (over z, y, x, core).
Axes of the slice: x: 2, y: 2, z: 4, core: 2. Of those that a mesh axis runs over, the one named last changes fastest.
Arguments:
- amplitudes: float32 [2, 512, 128, 512], P('runs', 'cfg')
- prop_third: float32 [2, 512, 512], replicated
- bitmasks_first: int32 [512], replicated, may hold values from 0 to 10922, as said below
- bitmasks_second: int32 [128], replicated, may hold values from 0 to 10922, as said below
- bitmasks_third: int32 [512], P('cfg'), may hold values from 0 to 10922, as said below
- detune_steps: int32 [3], P('runs'), may hold values from 0 to 15
Outputs:
- density: float32 [512, 2, 512], P(('runs', 'cfg'))
Inputs may be any that keep to these rules, and one draw needn't show every extreme that they name: `bitmasks_first`: 512 different numbers, none with two adjacent bits set. `bitmasks_second`: 128 different numbers, none with two adjacent bits set. `bitmasks_third`: 512 different numbers, none with two adjacent bits set.
All inputs are finite; a program needn't handle non-finite values.
Results may differ from a plain program's by a relative error of at most 0.00005.
Values sent between devices are 32-bit elements; how exact they have to be, the bound alone decides.
No kernel may reach another device: no remote copies, remote signals or barrier semaphores. Data moves between devices by JAX's collectives and lax.ppermute only.
A program may use at most 64 MiB of HBM per device.

v0:
```python
import jax
import jax.numpy as jnp
from jax import lax
from jax.sharding import PartitionSpec as P

angle_step = 0.2
pair_angle = 0.7
atom_count = 14


def atom_bit(bitmasks, which):
    return (jnp.right_shift(bitmasks, which) & 1).astype(jnp.float32)


def occupation(bitmasks):
    total = jnp.zeros(bitmasks.shape, jnp.float32)
    for which in range(atom_count):
        total = total + atom_bit(bitmasks, which)
    return total


def boundary_terms(first, second, third, detune_steps):
    scaled = detune_steps.astype(jnp.float32) * angle_step
    phase_first = scaled[0] * occupation(first)
    phase_second = scaled[1] * occupation(second)
    phase_third = scaled[2] * occupation(third)
    last_first = atom_bit(first, 13)[None, None, :]
    near_first = atom_bit(first, 12)[None, None, :]
    head_second = atom_bit(second, 0)[None, :, None]
    next_second = atom_bit(second, 1)[None, :, None]
    last_second = atom_bit(second, 13)[None, :, None]
    near_second = atom_bit(second, 12)[None, :, None]
    head_third = atom_bit(third, 0)[:, None, None]
    next_third = atom_bit(third, 1)[:, None, None]
    allowed = (1.0 - last_first * head_second) * (1.0 - last_second * head_third)
    pairs = (
        near_first * head_second
        + last_first * next_second
        + near_second * head_third
        + last_second * next_third
    )
    angle = (
        phase_third[:, None, None]
        + phase_second[None, :, None]
        + phase_first[None, None, :]
        + pair_angle * pairs
    )
    return (allowed, angle)


def apply_third(block, prop):

    def product(values, matrix):
        return jnp.einsum("ij,jba->iba", matrix, values, precision=lax.Precision.HIGHEST)

    real_part = product(block[0], prop[0]) - product(block[1], prop[1])
    imag_part = product(block[0], prop[1]) + product(block[1], prop[0])
    return jnp.stack([real_part, imag_part])


def inner_rows(left, right):
    return lax.dot_general(
        left,
        right,
        (((0,), (0,)), ((), ())),
        precision=lax.Precision.HIGHEST,
        preferred_element_type=jnp.float32,
    )


def shards(amplitudes, prop_third, bitmasks_first, bitmasks_second, bitmasks_third, detune_steps):
    allowed, angle = boundary_terms(bitmasks_first, bitmasks_second, bitmasks_third, detune_steps)
    cosine = jnp.cos(angle)
    sine = jnp.sin(angle)
    phased = jnp.stack(
        [
            allowed * (amplitudes[0] * cosine + amplitudes[1] * sine),
            allowed * (amplitudes[1] * cosine - amplitudes[0] * sine),
        ]
    )
    evolved = apply_third(
        lax.all_to_all(phased, "cfg", split_axis=2, concat_axis=1, tiled=True), prop_third
    )
    width = evolved.shape[3]
    flat_real = evolved[0].reshape(-1, width)
    flat_imag = evolved[1].reshape(-1, width)
    stacked = jnp.concatenate([flat_real, flat_imag], axis=0)
    local_real = inner_rows(stacked, stacked)
    crossed = inner_rows(flat_imag, flat_real)
    local_term = jnp.stack([local_real, crossed - crossed.T], axis=1)
    return lax.psum_scatter(local_term, "cfg", scatter_dimension=0, tiled=True)


def solution(mesh):
    placed = (P("runs", "cfg", None, None), P(), P(), P(), P("cfg"), P("runs"))
    return jax.shard_map(
        shards,
        mesh=mesh,
        in_specs=placed,
        out_specs=P(("runs", "cfg"), None, None),
        check_vma=False,
    )
```

profile of v0, /device:TPU:0, one launch (start us, length us, event | category | flops | bytes accessed | tf_op | source)
XLA Modules:
  0.0 469.0 jit_solution(2630011389610892652)
XLA Ops:
  6.5 0.0 reduce-scatter.2.cloned.1.call-start
  6.5 0.7 convert_multiply_fusion
  7.2 0.7 fusion.23
  7.8 0.7 and_convert_fusion.5
  8.5 1.3 add_multiply_fusion.2
  9.8 0.7 and_convert_fusion.7
  10.5 1.3 add_multiply_fusion.1
  11.8 0.7 and_convert_fusion.1
  12.5 1.3 add_multiply_fusion
  13.8 0.1 multiply_subtract_fusion.1
  13.9 0.1 copy.25
  14.0 0.1 copy.28
  14.1 0.1 copy.27
  14.2 4.5 fusion.22
  18.6 0.1 broadcast_add_fusion
  18.7 0.1 multiply_subtract_fusion
  18.9 18.9 %multiply_multiply_fusion.1 = (f32[1,16,128,512]{3,1,0,2:T(8,128)S(1)}, f32[1,16,128,512]{3,1,0,2:T(8,128)S(1)}) fusion(f32[1,16,128,512]{3,2,1,0:T(8,128)S(1)} %get-tuple-element.10, f32[1,16,128,512]{3,2,1,0:T(8,128)S(1)} %get-tuple-element.9, f32[16,128]{0,1:T(8,128)S(1)} %copy.28, f32[16,128]{0,1:T(8,128)S(1)} %copy.27, ...), kind=kLoop, calls=%fused_computation.7 | loop fusion | flops 14680064 | bytes 17336320 | tf_op jit(solution)/shard_map/mul | solution.py:77
  37.8 1.9 pad_maximum_fusion
  39.7 190.7 %all_to_all.15 = f32[2,16,128,512]{3,1,0,2:T(8,128)} all-to-all(f32[2,16,128,512]{3,1,0,2:T(8,128)S(1)} %pad_maximum_fusion), channel_id=1, replica_groups=mesh['runs'=1,'cfg'=32] {'cfg'}, dimensions={2} | all-to-all | bytes 16777216 | tf_op jit(solution)/shard_map/all_to_all | solution.py:82
  230.4 4.4 copy.44
  234.9 0.0 copy-start
  234.9 1.9 fusion.21
  236.8 0.0 copy-done
  236.8 8.0 %fusion.10 = f32[4,512,512]{1,2,0:T(8,128)S(1)} fusion(f32[512,4,512]{2,0,1:T(8,128)S(1)} %bitcast.43, f32[2,512,512]{2,1,0:T(8,128)S(1)} %copy-done), kind=kOutput, calls=%fused_computation.18 | convolution fusion | flops 6442450944 | bytes 9437184 | tf_op jit(solution)/shard_map/ij,jba->iba/dot_general | solution.py:54
  244.8 8.6 %fusion.14 = f32[4,512,512]{1,2,0:T(8,128)S(1)} fusion(f32[512,4,512]{2,0,1:T(8,128)S(1)} %bitcast.44, f32[2,512,512]{2,1,0:T(8,128)S(1)} %copy-done), kind=kOutput, calls=%fused_computation.22 | convolution fusion | flops 6442450944 | bytes 9437184 | tf_op jit(solution)/shard_map/ij,jba->iba/dot_general | solution.py:54
  253.5 9.1 %add_bitcast_fusion = f32[512,4,512]{2,0,1:T(8,128)S(1)} fusion(f32[4,512,512]{1,2,0:T(8,128)S(1)} %fusion.10, f32[512,4,512]{2,0,1:T(8,128)S(1)} %bitcast.41, f32[2,512,512]{2,1,0:T(8,128)S(1)} %copy-done), kind=kOutput, calls=%fused_computation.8 | convolution fusion | flops 6443499520 | bytes 13631488 | tf_op jit(solution)/shard_map/ij,jba->iba/dot_general | solution.py:54
  262.6 8.9 %subtract_bitcast_fusion = f32[512,4,512]{2,0,1:T(8,128)S(1)} fusion(f32[4,512,512]{1,2,0:T(8,128)S(1)} %fusion.14, f32[512,4,512]{2,0,1:T(8,128)S(1)} %bitcast.42, f32[2,512,512]{2,1,0:T(8,128)S(1)} %copy-done), kind=kOutput, calls=%fused_computation.9 | convolution fusion | flops 6443499520 | bytes 13631488 | tf_op jit(solution)/shard_map/ij,jba->iba/dot_general | solution.py:54
  271.5 4.7 copy.31
  276.2 7.5 %convolution_bitcast_fusion = f32[512,512]{1,0:T(8,128)S(1)} fusion(f32[512,4,512]{2,0,1:T(8,128)S(1)} %add_bitcast_fusion, f32[512,4,512]{2,0,1:T(8,128)S(1)} %subtract_bitcast_fusion), kind=kOutput, calls=%fused_computation.15 | convolution fusion | flops 6442450944 | bytes 9437184 | tf_op jit(solution)/shard_map/dot_general | solution.py:62
  283.7 4.6 copy.32
  288.3 5.3 %reshape_squeeze_stack.6 = f32[2048,512]{1,0:T(8,128)} reshape(f32[512,4,512]{2,1,0:T(4,128)} %copy.31) | data formatting | bytes 8388608 | tf_op jit(solution)/shard_map/reshape;squeeze;stack | solution.py:85
  293.6 5.3 %reshape_squeeze_stack.7 = f32[2048,512]{1,0:T(8,128)} reshape(f32[512,4,512]{2,1,0:T(4,128)} %copy.32) | data formatting | bytes 8388608 | tf_op jit(solution)/shard_map/reshape;squeeze;stack | solution.py:86
  299.0 0.3 copy.34
  299.3 0.2 fusion.9
  299.5 21.7 %fusion.6 = f32[512,1,512]{2,0,1:T(8,128)S(1)} fusion(f32[2048,512]{1,0:T(8,128)} %reshape_squeeze_stack.7, f32[2048,512]{1,0:T(8,128)} %reshape_squeeze_stack.6), kind=kOutput, calls=%fused_computation.14 | convolution fusion | flops 12886999040 | bytes 9437184 | tf_op jit(solution)/shard_map/dot_general | solution.py:62
  321.2 1.5 pad_maximum_fusion.1
  322.7 0.0 reduce-scatter.2.cloned.1.call-update
  322.8 137.7 %reduce-scatter.2.cloned.1.call-done = f32[16,2,512]{2,0,1:T(8,128)} async-done(((f32[512,2,512]{2,0,1:T(8,128)}), f32[16,2,512]{2,0,1:T(8,128)}) %reduce-scatter.2.cloned.1.call-update) | async-done | bytes 65552 | tf_op jit(solution)/shard_map/reduce_scatter | solution.py:91
  460.5 1.5 copy.35
Async XLA Ops:
  6.5 454.0 %reduce-scatter.2.cloned.1.call-start = ((), (), s32[]{:S(2)}) async-start(), calls=%async_computation.2 | async-start | bytes 2162688 | tf_op jit(solution)/shard_map/reduce_scatter | solution.py:91
  234.9 1.9 copy-start
Sparse Core Ops, SparseCore 0:
  322.9 137.5 reduce-scatter.1
where the time goes:
time: 478 us; the launch traced here: 469 us
  blocking collectives  191 us (40%)
  waiting for transfers between devices  138 us (29%)
  matrix products  63.8 us (13%)
  local copies, waits for them, and re-layouts  33.6 us (7%)
  other arithmetic  29.4 us (6%)
  between operations  13.7 us (3%)
    all_to_all x1, blocking collectives, shards(): lax.all_to_all(phased, 'cfg', split_axis=2, concat_axis=1, tiled=True)  191 us
    reduce_scatter x1, waiting for transfers between devices, shards(): return lax.psum_scatter(local_term, 'cfg', scatter_dimension=0, tiled=True)  138 us
    dot_general x4, matrix products, product(): jnp.einsum('ij,jba->iba', matrix, values, precision=lax.Precision.HIGHEST)  34.7 us
    dot_general x2, matrix products, inner_rows(): lax.dot_general(left, right, (((0,), (0,)), ((), ())), precision=lax.Prec...  29.2 us
    mul x1, other arithmetic, shards(): allowed * (amplitudes[0] * cosine + amplitudes[1] * sine)  18.9 us
  transfers between devices with their start and end apart: 1, of which 1 were waited for; matrix products, arithmetic and copies ran while one was open for 0% of the time, Pallas kernels for 0%

commit v1 on v0

--- a/solution.py
+++ b/solution.py
@@ -1,22 +1,204 @@
 import jax
 import jax.numpy as jnp
 from jax import lax
+from jax.experimental import pallas as pl
+from jax.experimental.pallas import tpu as pltpu
 from jax.sharding import PartitionSpec as P
 
 angle_step = 0.2
 pair_angle = 0.7
 atom_count = 14
-
-
-def atom_bit(bitmasks, which):
-    return (jnp.right_shift(bitmasks, which) & 1).astype(jnp.float32)
-
-
-def occupation(bitmasks):
-    total = jnp.zeros(bitmasks.shape, jnp.float32)
-    for which in range(atom_count):
-        total = total + atom_bit(bitmasks, which)
+tile = 128
+
+
+def bit(masks, which):
+    return (jnp.right_shift(masks, which) & 1).astype(jnp.float32)
+
+
+def occupation(masks):
+    total = bit(masks, 0)
+    for which in range(1, atom_count):
+        total = total + bit(masks, which)
     return total
+
+
+def high_low(values):
+    high = values.astype(jnp.bfloat16)
+    low = (values - high.astype(jnp.float32)).astype(jnp.bfloat16)
+    return high, low
+
+
+def pack_body(shape, steps, third, second_smem, first, second, amps, packed, row_re, row_im, col_re, col_im):
+    rows, seconds, owned, width = shape
+
+    @pl.when((pl.program_id(0) == 0) & (pl.program_id(1) == 0))
+    def tables():
+        scale_first = steps[0].astype(jnp.float32) * angle_step
+        scale_second = steps[1].astype(jnp.float32) * angle_step
+        scale_third = steps[2].astype(jnp.float32) * angle_step
+        kind = lax.broadcasted_iota(jnp.int32, (8, width), 0)
+        masks = jnp.broadcast_to(first[...], (8, width))
+        head = bit(kind, 0)
+        angle = scale_first * occupation(masks) + pair_angle * (
+            bit(masks, 12) * head + bit(masks, 13) * bit(kind, 1)
+        )
+        allowed = 1.0 - bit(masks, 13) * head
+        table_re = allowed * jnp.cos(angle)
+        table_im = -allowed * jnp.sin(angle)
+        for index in range(width // tile):
+            row_re[pl.ds(8 * index, 8), :] = table_re[:, index * tile : (index + 1) * tile]
+            row_im[pl.ds(8 * index, 8), :] = table_im[:, index * tile : (index + 1) * tile]
+        place = lax.broadcasted_iota(jnp.int32, (rows, seconds), 0)
+        masks_third = jnp.zeros((rows, seconds), jnp.int32)
+        for row in range(rows):
+            masks_third = jnp.where(place == row, third[row], masks_third)
+        masks_second = jnp.broadcast_to(second[...], (rows, seconds))
+        last = bit(masks_second, 13)
+        angle = (
+            scale_third * occupation(masks_third)
+            + scale_second * occupation(masks_second)
+            + pair_angle * (bit(masks_second, 12) * bit(masks_third, 0) + last * bit(masks_third, 1))
+        )
+        allowed = 1.0 - last * bit(masks_third, 0)
+        col_re[...] = allowed * jnp.cos(angle)
+        col_im[...] = -allowed * jnp.sin(angle)
+
+    here = pl.ds(pl.multiple_of(pl.program_id(0) * 8, 8), 8)
+    base = pl.program_id(1) * 8
+    columns_re = col_re[here, :]
+    columns_im = col_im[here, :]
+    for second_state in range(seconds):
+        kind = base + (second_smem[second_state] & 3)
+        across_re = row_re[pl.ds(kind, 1), :]
+        across_im = row_im[pl.ds(kind, 1), :]
+        down_re = columns_re[:, second_state : second_state + 1]
+        down_im = columns_im[:, second_state : second_state + 1]
+        turn_re = down_re * across_re - down_im * across_im
+        turn_im = down_re * across_im + down_im * across_re
+        real = amps[0, pl.ds(second_state, 8, stride=seconds), :]
+        imag = amps[1, pl.ds(second_state, 8, stride=seconds), :]
+        target, slot = second_state // owned, second_state % owned
+        lanes = pl.ds(slot * tile, tile)
+        packed[target, 0, :, lanes] = real * turn_re - imag * turn_im
+        packed[target, 1, :, lanes] = real * turn_im + imag * turn_re
+
+
+def pack(amps, first, second, third, steps, devices):
+    _, rows, seconds, width = amps.shape
+    owned = seconds // devices
+    smem = pl.BlockSpec(memory_space=pltpu.SMEM)
+    whole = lambda n: pl.BlockSpec((1, n), lambda i, j: (0, 0))
+    return pl.pallas_call(
+        lambda *refs: pack_body((rows, seconds, owned, width), *refs),
+        grid=(rows // 8, width // tile),
+        in_specs=[smem, smem, smem, whole(width), whole(seconds),
+                  pl.BlockSpec((2, 8 * seconds, tile), lambda i, j: (0, i, j))],
+        out_specs=pl.BlockSpec((devices, 2, 8, owned * tile), lambda i, j: (0, 0, i, j)),
+        out_shape=jax.ShapeDtypeStruct((devices, 2, rows, owned * width), jnp.float32),
+        scratch_shapes=[pltpu.VMEM((8 * width // tile, tile), jnp.float32)] * 2 + [pltpu.VMEM((rows, seconds), jnp.float32)] * 2,
+        compiler_params=pltpu.CompilerParams(dimension_semantics=("arbitrary", "arbitrary")),
+        name="pack",
+    )(steps, third, second, first.reshape(1, -1), second.reshape(1, -1), amps.reshape(2, rows * seconds, width))
+
+
+def density_body(parity_axis, tiles, prop, *refs):
+    parts = refs[:tiles]
+    keep, send, matrix, values, evolved, square, cross = refs[tiles:]
+    step = pl.program_id(0)
+    n = prop.shape[1]
+    width = tiles * tile
+
+    @pl.when(step == 0)
+    def prepare():
+        for plane, sign, row, column in ((0, 1, 0, 0), (1, -1, 0, 1), (1, 1, 1, 0), (0, 1, 1, 1)):
+            high, low = high_low(prop[plane])
+            if sign < 0:
+                high, low = -high, -low
+            rows = pl.ds(row * n, n)
+            matrix[rows, pl.ds(column * n, n)] = high
+            matrix[rows, pl.ds((2 + column) * n, n)] = high
+            matrix[rows, pl.ds((4 + column) * n, n)] = low
+        square[...] = jnp.zeros_like(square)
+        cross[...] = jnp.zeros_like(cross)
+
+    for plane in range(2):
+        for index, part in enumerate(parts):
+            high, low = high_low(part[:, plane].reshape(n, tile))
+            lanes = pl.ds(index * tile, tile)
+            values[pl.ds(plane * n, n), lanes] = high
+            values[pl.ds((2 + plane) * n, n), lanes] = low
+            values[pl.ds((4 + plane) * n, n), lanes] = high
+
+    block = 256
+
+    def evolve(index, carry):
+        rows = pl.ds(pl.multiple_of(index * block, block), block)
+        evolved[rows, :] = jnp.dot(matrix[rows, :], values[...], preferred_element_type=jnp.float32)
+        return carry
+
+    lax.fori_loop(0, 2 * n // block, evolve, 0)
+
+    high, low = high_low(evolved[...])
+    both = jnp.concatenate([high, low], axis=1)
+    turned_high = high.T
+    turned_low = low[n:].T
+    square[...] += jnp.dot(turned_high, both, preferred_element_type=jnp.float32)
+    cross[...] += (
+        jnp.dot(turned_high[:, n:], high[:n], preferred_element_type=jnp.float32)
+        + jnp.dot(turned_high[:, n:], low[:n], preferred_element_type=jnp.float32)
+        + jnp.dot(turned_low, high[:n], preferred_element_type=jnp.float32)
+    )
+
+    @pl.when(step == pl.num_programs(0) - 1)
+    def finish():
+        mixed = square[:, width:]
+        square[:, :width] = square[:, :width] + mixed + mixed.T
+        square[:, width:] = cross[...] - cross[...].T
+        parity = lax.rem(lax.axis_index(parity_axis), 2)
+        own = keep.shape[1]
+        for chip in range(keep.shape[0]):
+            near = pl.multiple_of((2 * chip + parity) * own, own)
+            far = pl.multiple_of((2 * chip + 1 - parity) * own, own)
+            keep[chip] = square[pl.ds(near, own), :]
+            send[chip] = square[pl.ds(far, own), :]
+
+
+def density(prop, parts, width, devices):
+    n = prop.shape[1]
+    sources, _, rows, lanes = parts.shape
+    own = width // devices
+    tiles, slots = width // tile, lanes // width
+    half = jax.ShapeDtypeStruct((devices // 2, own, 2 * width), jnp.float32)
+    fixed = pl.BlockSpec((devices // 2, own, 2 * width), lambda i: (0, 0, 0))
+    return pl.pallas_call(
+        lambda *refs: density_body("cfg", tiles, *refs),
+        grid=(slots,),
+        in_specs=[pl.BlockSpec((2, n, n), lambda i: (0, 0, 0)),
+                  *(pl.BlockSpec((sources, 2, rows, tile), lambda i, t=t: (0, 0, 0, t * slots + i)) for t in range(tiles))],
+        out_specs=(fixed, fixed),
+        out_shape=(half, half),
+        scratch_shapes=[
+            pltpu.VMEM((2 * n, 6 * n), jnp.bfloat16),
+            pltpu.VMEM((6 * n, width), jnp.bfloat16),
+            pltpu.VMEM((2 * n, width), jnp.float32),
+            pltpu.VMEM((width, 2 * width), jnp.float32),
+            pltpu.VMEM((width, width), jnp.float32),
+        ],
+        compiler_params=pltpu.CompilerParams(dimension_semantics=("arbitrary",), vmem_limit_bytes=60 * 2**20),
+        name="density",
+    )(prop, *[parts] * tiles)
+
+
+def shards(amplitudes, prop_third, first, second, third, steps, devices):
+    width = amplitudes.shape[3]
+    packed = pack(amplitudes, first, second, third, steps, devices)
+    parts = lax.all_to_all(packed, "cfg", split_axis=0, concat_axis=0, tiled=True)
+    keep, send = density(prop_third, parts, width, devices)
+    swap = [(i, i ^ 1) for i in range(devices)]
+    half = keep + lax.ppermute(send, "cfg", swap)
+    groups = [list(range(core, devices, 2)) for core in range(2)]
+    pieces = lax.all_to_all(half, "cfg", split_axis=0, concat_axis=0, tiled=True, axis_index_groups=groups)
+    return jnp.sum(pieces, axis=0).reshape(-1, 2, width)
 
 
 def boundary_terms(first, second, third, detune_steps):
@@ -24,14 +206,14 @@
     phase_first = scaled[0] * occupation(first)
     phase_second = scaled[1] * occupation(second)
     phase_third = scaled[2] * occupation(third)
-    last_first = atom_bit(first, 13)[None, None, :]
-    near_first = atom_bit(first, 12)[None, None, :]
-    head_second = atom_bit(second, 0)[None, :, None]
-    next_second = atom_bit(second, 1)[None, :, None]
-    last_second = atom_bit(second, 13)[None, :, None]
-    near_second = atom_bit(second, 12)[None, :, None]
-    head_third = atom_bit(third, 0)[:, None, None]
-    next_third = atom_bit(third, 1)[:, None, None]
+    last_first = bit(first, 13)[None, None, :]
+    near_first = bit(first, 12)[None, None, :]
+    head_second = bit(second, 0)[None, :, None]
+    next_second = bit(second, 1)[None, :, None]
+    last_second = bit(second, 13)[None, :, None]
+    near_second = bit(second, 12)[None, :, None]
+    head_third = bit(third, 0)[:, None, None]
+    next_third = bit(third, 1)[:, None, None]
     allowed = (1.0 - last_first * head_second) * (1.0 - last_second * head_third)
     pairs = (
         near_first * head_second
@@ -68,7 +250,7 @@
     )
 
 
-def shards(amplitudes, prop_third, bitmasks_first, bitmasks_second, bitmasks_third, detune_steps):
+def plain_shards(amplitudes, prop_third, bitmasks_first, bitmasks_second, bitmasks_third, detune_steps):
     allowed, angle = boundary_terms(bitmasks_first, bitmasks_second, bitmasks_third, detune_steps)
     cosine = jnp.cos(angle)
     sine = jnp.sin(angle)
@@ -92,9 +274,17 @@
 
 
 def solution(mesh):
+    devices = mesh.shape["cfg"]
+
+    def body(amplitudes, *others):
+        rows = amplitudes.shape[1]
+        if rows % 8 or amplitudes.shape[2] % devices or (amplitudes.shape[3] // devices) % 8 or amplitudes.shape[3] % tile:
+            return plain_shards(amplitudes, *others)
+        return shards(amplitudes, *others, devices)
+
     placed = (P("runs", "cfg", None, None), P(), P(), P(), P("cfg"), P("runs"))
     return jax.shard_map(
-        shards,
+        body,
         mesh=mesh,
         in_specs=placed,
         out_specs=P(("runs", "cfg"), None, None),

time: 478 us -> 271 us (0.57); the launches traced: 469 us -> 271 us
  waiting for transfers between devices: 138 us -> 2.87 us
  matrix products: 63.8 us -> 0 us
  Pallas kernels: 0 us -> 43.8 us
  local copies, waits for them, and re-layouts: 33.6 us -> 0.69 us
  blocking collectives: 191 us -> 222 us
  other arithmetic: 29.4 us -> 1.42 us
  between operations: 13.7 us -> 0.01 us
    reduce_scatter x1 -> x0, waiting for transfers between devices: 138 us -> none  [shards(): return lax.psum_scatter(local_term, 'cfg', scatter_dimension=0, tiled=True)]
    dot_general x6 -> x0, matrix products: 63.8 us -> none  [the longest x4 34.7 us: product(): jnp.einsum('ij,jba->iba', matrix, values, precision=lax.Precision.HIGHEST)]
    pallas_call x0 -> x2, Pallas kernels: none -> 43.8 us  [the longest x1 32.4 us: density(): pl.pallas_call(lambda *refs: density_body('cfg', tiles, *refs), grid=(slo...]
    all_to_all x1 -> x2, blocking collectives: 191 us -> 222 us  [the longest x1 191 us: shards(): lax.all_to_all(packed, 'cfg', split_axis=0, concat_axis=0, tiled=True)]
    mul x5 -> x0, other arithmetic: 23.5 us -> none  [the longest x1 18.9 us: shards(): allowed * (amplitudes[0] * cosine + amplitudes[1] * sine)]
    another operation x2 -> x0, local copies, waits for them, and re-layouts: 10.6 us -> none  [the longest x1 5.32 us: shards(): flat_imag = evolved[1].reshape(-1, width)]
    slice x3 -> x0, local copies, waits for them, and re-layouts: 7.02 us -> none  [the longest x1 4.46 us: shards(): amplitudes[0] * cosine + amplitudes[1] * sine]
where the time goes in v1:
time: 271 us
  blocking collectives  222 us (82%)
  Pallas kernels  43.8 us (16%)
  waiting for transfers between devices  2.87 us (1%)
    all_to_all x1, blocking collectives, shards(): lax.all_to_all(packed, 'cfg', split_axis=0, concat_axis=0, tiled=True)  191 us
    pallas_call x1, Pallas kernels, density(): pl.pallas_call(lambda *refs: density_body('cfg', tiles, *refs), grid=(slo...  32.4 us
    all_to_all x1, blocking collectives, shards(): lax.all_to_all(half, 'cfg', split_axis=0, concat_axis=0, tiled=True, axis...  31.2 us
    pallas_call x1, Pallas kernels, pack(): pl.pallas_call(lambda *refs: pack_body((rows, seconds, owned, width), *re...  11.3 us
  transfers between devices with their start and end apart: 1, of which 1 were waited for; matrix products, arithmetic and copies ran while one was open for 0% of the time, Pallas kernels for 0%

profile of v1, /device:TPU:0, one launch (start us, length us, event | category | flops | bytes accessed | tf_op | source)
XLA Modules:
  0.0 270.9 jit_solution(12645319992133585347)
XLA Ops:
  0.0 11.3 %pack.1 = f32[32,2,16,2048]{3,2,1,0:T(8,128)} custom-call(s32[3]{0:T(128)} %refs_0_.2, s32[16]{0:T(128)} %refs_1_.1, s32[128]{0:T(128)} %refs_2_.1, s32[1,512]{1,0:T(1,128)} %bitcast.5, s32[1,128]{1,0:T(1,128)} %bitcast.4, f32[2,2048,512]{2,1,0:T(8,128)} %bitcast.3), custom_call_target="tpu_custom_call" | custom-call | tf_op jit(solution)/shard_map/pack/pallas_call | solution.py:91
  11.3 190.9 %all_to_all.10.refs_1_.refs_2_.refs_3_.refs_4_ = f32[32,2,16,2048]{3,2,1,0:T(8,128)} all-to-all(f32[32,2,16,2048]{3,2,1,0:T(8,128)} %pack.1), channel_id=1, replica_groups=mesh['runs'=1,'cfg'=32] {'cfg'}, dimensions={0} | all-to-all | bytes 16777216 | tf_op jit(solution)/shard_map/all_to_all | solution.py:195
  202.2 32.4 %density.1 = (f32[16,16,1024]{2,1,0:T(8,128)}, f32[16,16,1024]{2,1,0:T(8,128)}) custom-call(f32[2,512,512]{2,1,0:T(8,128)} %refs_0_.3, f32[32,2,16,2048]{3,2,1,0:T(8,128)} %all_to_all.10.refs_1_.refs_2_.refs_3_.refs_4_, f32[32,2,16,2048]{3,2,1,0:T(8,128)} %all_to_all.10.refs_1_.refs_2_.refs_3_.refs_4_, ...), custom_call_target="tpu_custom_call" | custom-call | tf_op jit(solution)/shard_map/density/pallas_call | solution.py:173
  234.7 0.0 collective-permute-start
  234.7 2.9 %collective-permute-done = f32[16,16,1024]{2,1,0:T(8,128)S(1)} collective-permute-done((f32[16,16,1024]{2,1,0:T(8,128)}, f32[16,16,1024]{2,1,0:T(8,128)S(1)}, u32[]{:S(2)}, u32[]{:S(2)}) %collective-permute-start) | collective-permute-done | bytes 1048608 | tf_op jit(solution)/shard_map/ppermute | solution.py:198
  237.6 1.4 add.3
  238.9 31.2 %all_to_all.11 = f32[16,16,1024]{2,1,0:T(8,128)S(1)} all-to-all(f32[16,16,1024]{2,1,0:T(8,128)S(1)} %add.3), channel_id=1, replica_groups={{0,2,4,6,8,10,12,14,16,18,20,22,24,26,28,30},{1,3,5,7,9,11,13,15,17,19,..., dimensions={0} | all-to-all | bytes 2097152 | tf_op jit(solution)/shard_map/all_to_all | solution.py:200
  270.1 0.1 reduce_sum.9
  270.2 0.7 reshape.15
Async XLA Ops:
  234.7 2.9 %collective-permute-start = (f32[16,16,1024]{2,1,0:T(8,128)}, f32[16,16,1024]{2,1,0:T(8,128)S(1)}, u32[]{:S(2)}, u32[]{:S(2)}) collective-permute-start(f32[16,16,1024]{2,1,0:T(8,128)} %get-tuple-element.8), channel_id=1, source_target_pairs={{0,1},{1,0},{2,3},{3,2},{4,5},{5,4},{6,7},{7,6},{8,9},{9,8},{10,11... | collective-permute-start | bytes 3145736 | tf_op jit(solution)/shard_map/ppermute | solution.py:198

commit v2 on v1

v2 whole, which is shorter than its diff:
```python
import jax
import jax.numpy as jnp
from jax import lax
from jax.experimental import pallas as pl
from jax.experimental.pallas import tpu as pltpu
from jax.sharding import PartitionSpec as P

angle_step = 0.2
pair_angle = 0.7
atom_count = 14
tile = 128


def bit(masks, which):
    return (jnp.right_shift(masks, which) & 1).astype(jnp.float32)


def occupation(masks):
    total = bit(masks, 0)
    for which in range(1, atom_count):
        total = total + bit(masks, which)
    return total


def high_low(values):
    high = values.astype(jnp.bfloat16)
    low = (values - high.astype(jnp.float32)).astype(jnp.bfloat16)
    return high, low


def swapped_lanes(values, distance):
    lanes = values.shape[1]
    place = lax.broadcasted_iota(jnp.int32, values.shape, 1)
    up = pltpu.roll(values, lanes - distance, 1)
    down = pltpu.roll(values, distance, 1)
    return jnp.where((place & distance) == 0, up, down)


def pack_body(shape, first_slot, group, place_smem, steps, third, second_smem, first, second, *refs):
    rows, seconds, owned, width, devices, members, slots = shape
    mixed = group is not None
    tiles = width // tile
    amps = [ref.reshape(2, rows * members * owned, tile) for ref in refs[:tiles]]
    row_re, row_im, col_re, col_im = refs[-4:]
    packed = refs[tiles:-4]
    me = place_smem[0] & (members - 1) if mixed else 0
    offset = place_smem[1] * (members * owned) if mixed else 0

    def tables():
        scale_first = steps[0].astype(jnp.float32) * angle_step
        scale_second = steps[1].astype(jnp.float32) * angle_step
        scale_third = steps[2].astype(jnp.float32) * angle_step
        kind = lax.broadcasted_iota(jnp.int32, (8, width), 0)
        masks = jnp.broadcast_to(first[...], (8, width))
        head = bit(kind, 0)
        angle = scale_first * occupation(masks) + pair_angle * (
            bit(masks, 12) * head + bit(masks, 13) * bit(kind, 1)
        )
        allowed = 1.0 - bit(masks, 13) * head
        table_re = allowed * jnp.cos(angle)
        table_im = -allowed * jnp.sin(angle)
        for index in range(tiles):
            row_re[pl.ds(8 * index, 8), :] = table_re[:, index * tile : (index + 1) * tile]
            row_im[pl.ds(8 * index, 8), :] = table_im[:, index * tile : (index + 1) * tile]
        place = lax.broadcasted_iota(jnp.int32, (rows, seconds), 0)
        masks_third = jnp.zeros((rows, seconds), jnp.int32)
        for row in range(rows):
            masks_third = jnp.where(place == row, third[row], masks_third)
        masks_second = jnp.broadcast_to(second[...], (rows, seconds))
        if mixed:
            distance, change = 1, place_smem[2]
            while distance < devices:
                masks_second = jnp.where(
                    (change & distance) != 0, swapped_lanes(masks_second, distance * owned), masks_second
                )
                distance *= 2
        last = bit(masks_second, 13)
        angle = (
            scale_third * occupation(masks_third)
            + scale_second * occupation(masks_second)
            + pair_angle * (bit(masks_second, 12) * bit(masks_third, 0) + last * bit(masks_third, 1))
        )
        allowed = 1.0 - last * bit(masks_third, 0)
        col_re[...] = allowed * jnp.cos(angle)
        col_im[...] = -allowed * jnp.sin(angle)

    tables()
    stride = members * owned
    for target in range(members):
        for slot in range(first_slot, first_slot + slots):
            state = (me ^ target) * owned + slot
            kind = second_smem[offset + state] & 3
            column = target * owned + slot
            out = packed[target] if mixed else packed[0].at[target]
            for half in range(0, rows, 8):
                down_re = col_re[pl.ds(half, 8), column : column + 1]
                down_im = col_im[pl.ds(half, 8), column : column + 1]
                for index in range(tiles):
                    across_re = row_re[pl.ds(8 * index + kind, 1), :]
                    across_im = row_im[pl.ds(8 * index + kind, 1), :]
                    turn_re = down_re * across_re - down_im * across_im
                    turn_im = down_re * across_im + down_im * across_re
                    real = amps[index][0, pl.ds(half * stride + state, 8, stride=stride), :]
                    imag = amps[index][1, pl.ds(half * stride + state, 8, stride=stride), :]
                    lanes = pl.ds((slot - first_slot) * width + index * tile, tile)
                    out[0, pl.ds(half, 8), lanes] = real * turn_re - imag * turn_im
                    out[1, pl.ds(half, 8), lanes] = real * turn_im + imag * turn_re


def pack(amps, first, second, third, steps, devices, first_slot, slots, group, members):
    _, rows, seconds, width = amps.shape
    tiles = width // tile
    owned = seconds // devices
    smem = pl.BlockSpec(memory_space=pltpu.SMEM)
    whole = lambda n: pl.BlockSpec((1, n), lambda i, at: (0, 0))
    if group is not None:
        out_specs = tuple(pl.BlockSpec((2, rows, slots * width), lambda i, at: (0, 0, 0)) for _ in range(members))
        out_shape = tuple(jax.ShapeDtypeStruct((2, rows, slots * width), jnp.float32) for _ in range(members))
        me = lax.axis_index("cfg")
        plane = jnp.right_shift(me, members.bit_length() - 1) ^ group
        place = jnp.stack([me, plane, me ^ (group * members)])
    else:
        members = devices
        out_specs = pl.BlockSpec((devices, 2, rows, slots * width), lambda i, at: (0, 0, 0, 0))
        out_shape = jax.ShapeDtypeStruct((devices, 2, rows, slots * width), jnp.float32)
        place = jnp.zeros((3,), jnp.int32)
    shape = (rows, seconds, owned, width, devices, members, slots)
    return pl.pallas_call(
        lambda *refs: pack_body(shape, first_slot, group, *refs),
        grid_spec=pltpu.PrefetchScalarGridSpec(
            num_scalar_prefetch=1,
            grid=(1,),
            in_specs=[smem, smem, smem, whole(width), whole(seconds),
                      *(pl.BlockSpec((2, rows, members * owned, tile), lambda i, at, t=t: (0, 0, at[1], t)) for t in range(tiles))],
            out_specs=out_specs,
            scratch_shapes=[pltpu.VMEM((8 * tiles, tile), jnp.float32)] * 2 + [pltpu.VMEM((rows, seconds), jnp.float32)] * 2,
        ),
        out_shape=out_shape,
        compiler_params=pltpu.CompilerParams(dimension_semantics=("arbitrary",)),
        cost_estimate=pl.CostEstimate(flops=24 * amps.size, bytes_accessed=8 * amps.size, transcendentals=0),
    )(place, steps, third, second, first.reshape(1, -1), second.reshape(1, -1), *[amps] * tiles)


def spread_propagator(prop, matrix):
    n = prop.shape[1]
    for plane, sign, row, column in ((0, 1, 0, 0), (1, -1, 0, 1), (1, 1, 1, 0), (0, 1, 1, 1)):
        high, low = high_low(prop[plane])
        if sign < 0:
            high, low = -high, -low
        rows = pl.ds(row * n, n)
        matrix[rows, pl.ds(column * n, n)] = high
        matrix[rows, pl.ds((2 + column) * n, n)] = low


def add_block(matrix, values, evolved, sums, ready=None):
    n = matrix.shape[0] // 2
    width = sums.shape[0]
    square, cross = sums.at[:, pl.ds(0, 2 * width)], sums.at[:, pl.ds(2 * width, width)]
    block = 256

    def evolve(index, carry):
        rows = pl.ds(pl.multiple_of(index * block, block), block)
        high = matrix[rows, pl.ds(0, 2 * n)]
        low = matrix[rows, pl.ds(2 * n, 2 * n)]
        evolved[rows, :] = (
            jnp.dot(high, values[pl.ds(0, 2 * n), :], preferred_element_type=jnp.float32)
            + jnp.dot(high, values[pl.ds(2 * n, 2 * n), :], preferred_element_type=jnp.float32)
            + jnp.dot(low, values[pl.ds(0, 2 * n), :], preferred_element_type=jnp.float32)
        )
        return carry

    lax.fori_loop(0, 2 * n // block, evolve, 0)
    if ready is not None:
        ready()
    high, low = high_low(evolved[...])
    both = jnp.concatenate([high, low], axis=1)
    turned_high = high.T
    turned_low = low[n:].T
    square[...] += jnp.dot(turned_high, both, preferred_element_type=jnp.float32)
    cross[...] += (
        jnp.dot(turned_high[:, n:], high[:n], preferred_element_type=jnp.float32)
        + jnp.dot(turned_high[:, n:], low[:n], preferred_element_type=jnp.float32)
        + jnp.dot(turned_low, high[:n], preferred_element_type=jnp.float32)
    )


def fill(values, n, plane, start, rows, block):
    high, low = high_low(block)
    values[pl.ds(plane * n + start, rows), :] = high
    values[pl.ds((2 + plane) * n + start, rows), :] = low


def density_early_body(count, prop, *refs):
    parts, (sums, matrix, values, evolved) = refs[:count], refs[count:]
    n = prop.shape[1]

    @pl.when(pl.program_id(0) == 0)
    def prepare():
        spread_propagator(prop, matrix)
        sums[...] = jnp.zeros_like(sums)

    me = lax.axis_index("cfg")
    for plane in range(2):
        for index, part in enumerate(parts):
            rows = part.shape[1]
            fill(values, n, plane, pl.multiple_of((me ^ index) * rows, rows), rows, part[plane])
    add_block(matrix, values, evolved, sums)


def density_late_body(matrix_far, parts, sums_far, keep, send, matrix, values, evolved, sums, sems):
    n = matrix.shape[0] // 2
    width = sums.shape[0]
    copies = [
        pltpu.make_async_copy(matrix_far, matrix, sems.at[0]),
        pltpu.make_async_copy(sums_far, sums, sems.at[1]),
    ]
    for copy in copies:
        copy.start()
    for plane in range(2):
        fill(values, n, plane, 0, n, parts[:, plane].reshape(n, width))
    copies[0].wait()

    add_block(matrix, values, evolved, sums, copies[1].wait)
    mixed = sums[:, width : 2 * width]
    cross = sums[:, 2 * width :]
    sums[:, :width] = sums[:, :width] + mixed + mixed.T
    sums[:, width : 2 * width] = cross - cross.T
    parity = lax.rem(lax.axis_index("cfg"), 2)
    own = keep.shape[1]
    for chip in range(keep.shape[0]):
        near = pl.multiple_of((2 * chip + parity) * own, own)
        far = pl.multiple_of((2 * chip + 1 - parity) * own, own)
        keep[chip] = sums[pl.ds(near, own), pl.ds(0, 2 * width)]
        send[chip] = sums[pl.ds(far, own), pl.ds(0, 2 * width)]


def cost(slots, width, n):
    return pl.CostEstimate(flops=slots * width * n * (24 * n + 14 * width), bytes_accessed=2**24, transcendentals=0)


vmem = pl.BlockSpec(memory_space=pltpu.VMEM)
far = pl.BlockSpec(memory_space=pltpu.HBM)


def density_early(prop, parts, width):
    n = prop.shape[1]
    slots = parts[0].shape[-1] // width
    return pl.pallas_call(
        lambda *refs: density_early_body(len(parts), *refs),
        grid=(slots,),
        in_specs=[pl.BlockSpec((2, n, n), lambda i: (0, 0, 0)),
                  *(pl.BlockSpec((2, part.shape[1], width), lambda i: (0, 0, i)) for part in parts)],
        out_specs=(
            pl.BlockSpec((width, 3 * width), lambda i: (0, 0)),
            pl.BlockSpec((2 * n, 4 * n), lambda i: (0, 0)),
        ),
        out_shape=(
            jax.ShapeDtypeStruct((width, 3 * width), jnp.float32),
            jax.ShapeDtypeStruct((2 * n, 4 * n), jnp.bfloat16),
        ),
        scratch_shapes=[
            pltpu.VMEM((4 * n, width), jnp.bfloat16),
            pltpu.VMEM((2 * n, width), jnp.float32),
        ],
        compiler_params=pltpu.CompilerParams(dimension_semantics=("arbitrary",)),
        cost_estimate=cost(slots, width, n),
        name="density_early",
    )(prop, *parts)


def density_late(matrix, parts, sums, devices):
    n = matrix.shape[0] // 2
    width = sums.shape[0]
    half = jax.ShapeDtypeStruct((devices // 2, width // devices, 2 * width), jnp.float32)
    return pl.pallas_call(
        density_late_body,
        in_specs=[far, vmem, far],
        out_specs=(vmem, vmem),
        out_shape=(half, half),
        scratch_shapes=[
            pltpu.VMEM(matrix.shape, jnp.bfloat16),
            pltpu.VMEM((4 * n, width), jnp.bfloat16),
            pltpu.VMEM((2 * n, width), jnp.float32),
            pltpu.VMEM((width, 3 * width), jnp.float32),
            pltpu.SemaphoreType.DMA((2,)),
        ],
        compiler_params=pltpu.CompilerParams(vmem_limit_bytes=48 * 2**20),
        cost_estimate=cost(1, width, n),
        name="density_late",
    )(matrix, parts, sums)


def exchange_order(devices):
    half = devices // 2
    return list(range(half, devices)) + list(range(1, half))


def shards(amplitudes, prop_third, first, second, third, steps, devices):
    width = amplitudes.shape[3]
    owned = amplitudes.shape[2] // devices
    late = 1
    members = devices // 4
    arrived = [None] * devices
    blocks = []
    for group in range(4):
        blocks += pack(amplitudes, first, second, third, steps, devices, 0, owned - late, group, members)
    arrived[0] = blocks[0]
    for distance in exchange_order(devices):
        pairs = [(i, i ^ distance) for i in range(devices)]
        arrived[distance] = lax.ppermute(blocks[distance], "cfg", pairs)
    packed = pack(amplitudes, first, second, third, steps, devices, owned - late, late, None, None)
    parts = lax.all_to_all(packed, "cfg", split_axis=0, concat_axis=0, tiled=True)
    sums, matrix = density_early(prop_third, arrived, width)
    keep, send = density_late(matrix, parts, sums, devices)
    swap = [(i, i ^ 1) for i in range(devices)]
    half = keep + lax.ppermute(send, "cfg", swap)
    groups = [list(range(core, devices, 2)) for core in range(2)]
    pieces = lax.all_to_all(half, "cfg", split_axis=0, concat_axis=0, tiled=True, axis_index_groups=groups)
    return jnp.sum(pieces, axis=0).reshape(-1, 2, width)


def boundary_terms(first, second, third, detune_steps):
    scaled = detune_steps.astype(jnp.float32) * angle_step
    phase_first = scaled[0] * occupation(first)
    phase_second = scaled[1] * occupation(second)
    phase_third = scaled[2] * occupation(third)
    last_first = bit(first, 13)[None, None, :]
    near_first = bit(first, 12)[None, None, :]
    head_second = bit(second, 0)[None, :, None]
    next_second = bit(second, 1)[None, :, None]
    last_second = bit(second, 13)[None, :, None]
    near_second = bit(second, 12)[None, :, None]
    head_third = bit(third, 0)[:, None, None]
    next_third = bit(third, 1)[:, None, None]
    allowed = (1.0 - last_first * head_second) * (1.0 - last_second * head_third)
    pairs = (
        near_first * head_second
        + last_first * next_second
        + near_second * head_third
        + last_second * next_third
    )
    angle = (
        phase_third[:, None, None]
        + phase_second[None, :, None]
        + phase_first[None, None, :]
        + pair_angle * pairs
    )
    return (allowed, angle)


def apply_third(block, prop):

    def product(values, matrix):
        return jnp.einsum("ij,jba->iba", matrix, values, precision=lax.Precision.HIGHEST)

    real_part = product(block[0], prop[0]) - product(block[1], prop[1])
    imag_part = product(block[0], prop[1]) + product(block[1], prop[0])
    return jnp.stack([real_part, imag_part])


def inner_rows(left, right):
    return lax.dot_general(
        left,
        right,
        (((0,), (0,)), ((), ())),
        precision=lax.Precision.HIGHEST,
        preferred_element_type=jnp.float32,
    )


def plain_shards(amplitudes, prop_third, bitmasks_first, bitmasks_second, bitmasks_third, detune_steps):
    allowed, angle = boundary_terms(bitmasks_first, bitmasks_second, bitmasks_third, detune_steps)
    cosine = jnp.cos(angle)
    sine = jnp.sin(angle)
    phased = jnp.stack(
        [
            allowed * (amplitudes[0] * cosine + amplitudes[1] * sine),
            allowed * (amplitudes[1] * cosine - amplitudes[0] * sine),
        ]
    )
    evolved = apply_third(
        lax.all_to_all(phased, "cfg", split_axis=2, concat_axis=1, tiled=True), prop_third
    )
    width = evolved.shape[3]
    flat_real = evolved[0].reshape(-1, width)
    flat_imag = evolved[1].reshape(-1, width)
    stacked = jnp.concatenate([flat_real, flat_imag], axis=0)
    local_real = inner_rows(stacked, stacked)
    crossed = inner_rows(flat_imag, flat_real)
    local_term = jnp.stack([local_real, crossed - crossed.T], axis=1)
    return lax.psum_scatter(local_term, "cfg", scatter_dimension=0, tiled=True)


def solution(mesh):
    devices = mesh.shape["cfg"]

    def body(amplitudes, *others):
        rows = amplitudes.shape[1]
        seconds, width = amplitudes.shape[2:]
        powers = devices & (devices - 1) == 0
        if rows % 16 or seconds != tile or seconds // devices < 2 or (width // devices) % 8 or width % tile or not powers:
            return plain_shards(amplitudes, *others)
        return shards(amplitudes, *others, devices)

    placed = (P("runs", "cfg", None, None), P(), P(), P(), P("cfg"), P("runs"))
    return jax.shard_map(
        body,
        mesh=mesh,
        in_specs=placed,
        out_specs=P(("runs", "cfg"), None, None),
        check_vma=False,
    )
```

time: 271 us -> 315 us (1.16)
  blocking collectives: 222 us -> 32 us
  waiting for transfers between devices: 2.87 us -> 129 us
  starting transfers between devices: 0.01 us -> 87.5 us
  Pallas kernels: 43.8 us -> 62.2 us
    all_to_all x1 -> x0, blocking collectives: 191 us -> none  [shards(): lax.all_to_all(packed, 'cfg', split_axis=0, concat_axis=0, tiled=True)]
    ppermute x0 -> x31, waiting for transfers between devices: none -> 126 us  [shards(): arrived[distance] = lax.ppermute(blocks[distance], 'cfg', pairs)]
    ppermute x0 -> x31, starting transfers between devices: none -> 80 us  [shards(): arrived[distance] = lax.ppermute(blocks[distance], 'cfg', pairs)]
    pallas_call x2 -> x7, Pallas kernels: 43.8 us -> 62.2 us  [the longest x5 28.9 us: pack(): pl.pallas_call(lambda *refs: pack_body(shape, first_slot, group, *refs),...]
    all_to_all x0 -> x1, starting transfers between devices: none -> 7.51 us  [shards(): lax.all_to_all(packed, 'cfg', split_axis=0, concat_axis=0, tiled=True)]
  transfers between devices with their start and end apart: 1 -> 33, of which waited for: 1 -> 15; matrix products, arithmetic and copies ran while one was open for 0% -> 0% of each run, Pallas kernels for 0% -> 14%
where the time goes in v2:
time: 315 us
  waiting for transfers between devices  129 us (41%)
  starting transfers between devices  87.5 us (28%)
  Pallas kernels  62.2 us (20%)
  blocking collectives  32 us (10%)
    ppermute x31, waiting for transfers between devices, shards(): arrived[distance] = lax.ppermute(blocks[distance], 'cfg', pairs)  126 us
    ppermute x31, starting transfers between devices, shards(): arrived[distance] = lax.ppermute(blocks[distance], 'cfg', pairs)  80 us
    all_to_all x1, blocking collectives, shards(): lax.all_to_all(half, 'cfg', split_axis=0, concat_axis=0, tiled=True, axis...  32 us
    pallas_call x5, Pallas kernels, pack(): pl.pallas_call(lambda *refs: pack_body(shape, first_slot, group, *refs),...  28.9 us
    pallas_call x1, Pallas kernels, density_early(): pl.pallas_call(lambda *refs: density_early_body(len(parts), *refs), grid=...  24.2 us
    pallas_call x1, Pallas kernels, density_late(): pl.pallas_call(density_late_body, in_specs=[far, vmem, far], out_specs=(v...  9.15 us
    all_to_all x1, starting transfers between devices, shards(): lax.all_to_all(packed, 'cfg', split_axis=0, concat_axis=0, tiled=True)  7.51 us
  transfers between devices with their start and end apart: 33, of which 15 were waited for; matrix products, arithmetic and copies ran while one was open for 0% of the time, Pallas kernels for 14%

profile of v2, /device:TPU:0, one launch (start us, length us, event | category | flops | bytes accessed | tf_op | source)
XLA Modules:
  0.0 314.5 jit_solution(8665360547719302012)
XLA Ops:
  0.5 7.6 %shard_map.68 = f32[32,2,16,512]{3,2,1,0:T(8,128)} custom-call(s32[3]{0:T(128)} %broadcast_1_refs_0_.2.refs_0_, s32[3]{0:T(128)} %refs_1_.9, s32[16]{0:T(128)} %refs_2_.9, s32[128]{0:T(128)} %refs_3_.9, s32[1,512]{1,0:T(1,128)} %bitcast.10, s32[1,128]{1,0:T(1,128)} %bitcast.15, f32[2,16,128,512]{3,2,1,0:T(8,128)} %refs_9_.9, f32[2,16,128,512]{3,2,1,0:T(8,128)} %refs_9_.9, ...), custom_call_target="tpu_custom_call" | custom-call | flops 50331648 | bytes 16777216 | tf_op jit(solution)/shard_map/pallas_call | solution.py:128
  8.1 7.5 %all-to-all-start = ((f32[32,2,16,512]{3,2,1,0:T(8,128)}), f32[32,2,16,512]{3,2,1,0:T(8,128)S(1)}, u32[]{:S(2)}, u32[]{:S(2)}) async-start(f32[32,2,16,512]{3,2,1,0:T(8,128)} %shard_map.68), calls=%async_computation | async-start | bytes 4194304 | tf_op jit(solution)/shard_map/all_to_all | solution.py:312
  16.3 5.3 %shard_map.66 = (f32[2,16,1536]{2,1,0:T(8,128)}, f32[2,16,1536]{2,1,0:T(8,128)}, f32[2,16,1536]{2,1,0:T(8,128)}, f32[2,16,1536]{2,1,0:T(8,128)}, f32[2,16,1536]{...) custom-call(s32[3]{0:T(128)} %get-tuple-element.79.refs_0_, s32[3]{0:T(128)} %refs_1_.9, ...), custom_call_target="tpu_custom_call" | custom-call | flops 50331648 | bytes 16777216 | tf_op jit(solution)/shard_map/pallas_call | solution.py:128
  21.6 2.5 collective-permute-start.15
  24.1 3.3 %collective-permute-start.17 = (f32[2,16,1536]{2,1,0:T(8,128)}, f32[2,16,1536]{2,1,0:T(8,128)S(1)}, u32[]{:S(2)}, u32[]{:S(2)}) collective-permute-start(f32[2,16,1536]{2,1,0:T(8,128)} %get-tuple-element.59), channel_id=1, source_target_pairs={{0,18},{1,19},{2,16},{3,17},{4,22},{5,23},{6,20},{7,21},{8,26},{9,... | collective-permute-start | bytes 589832 | tf_op jit(solution)/shard_map/ppermute | solution.py:310
  27.7 3.4 %collective-permute-start.19 = (f32[2,16,1536]{2,1,0:T(8,128)}, f32[2,16,1536]{2,1,0:T(8,128)S(1)}, u32[]{:S(2)}, u32[]{:S(2)}) collective-permute-start(f32[2,16,1536]{2,1,0:T(8,128)} %get-tuple-element.61), channel_id=1, source_target_pairs={{0,20},{1,21},{2,22},{3,23},{4,16},{5,17},{6,18},{7,19},{8,28},{9,... | collective-permute-start | bytes 589832 | tf_op jit(solution)/shard_map/ppermute | solution.py:310
  31.2 59.0 %collective-permute-done.15.refs_17_ = f32[2,16,1536]{2,1,0:T(8,128)S(1)} collective-permute-done((f32[2,16,1536]{2,1,0:T(8,128)}, f32[2,16,1536]{2,1,0:T(8,128)S(1)}, u32[]{:S(2)}, u32[]{:S(2)}) %collective-permute-start.15) | collective-permute-done | bytes 196640 | tf_op jit(solution)/shard_map/ppermute | solution.py:310
  90.2 5.3 %shard_map.67 = (f32[2,16,1536]{2,1,0:T(8,128)}, f32[2,16,1536]{2,1,0:T(8,128)}, f32[2,16,1536]{2,1,0:T(8,128)}, f32[2,16,1536]{2,1,0:T(8,128)}, f32[2,16,1536]{...) custom-call(s32[3]{0:T(128)} %get-tuple-element.80.refs_0_, s32[3]{0:T(128)} %refs_1_.9, ...), custom_call_target="tpu_custom_call" | custom-call | flops 50331648 | bytes 16777216 | tf_op jit(solution)/shard_map/pallas_call | solution.py:128
  95.5 2.0 collective-permute-done.16.refs_18_
  97.4 2.5 collective-permute-start.21
  100.0 12.1 %collective-permute-done.17.refs_19_ = f32[2,16,1536]{2,1,0:T(8,128)S(1)} collective-permute-done((f32[2,16,1536]{2,1,0:T(8,128)}, f32[2,16,1536]{2,1,0:T(8,128)S(1)}, u32[]{:S(2)}, u32[]{:S(2)}) %collective-permute-start.17) | collective-permute-done | bytes 196640 | tf_op jit(solution)/shard_map/ppermute | solution.py:310
  112.0 3.1 collective-permute-done.18.refs_20_
  115.1 5.2 %collective-permute-done.19.refs_21_ = f32[2,16,1536]{2,1,0:T(8,128)S(1)} collective-permute-done((f32[2,16,1536]{2,1,0:T(8,128)}, f32[2,16,1536]{2,1,0:T(8,128)S(1)}, u32[]{:S(2)}, u32[]{:S(2)}) %collective-permute-start.19) | collective-permute-done | bytes 196640 | tf_op jit(solution)/shard_map/ppermute | solution.py:310
  120.4 11.5 %collective-permute-done.20.refs_22_ = f32[2,16,1536]{2,1,0:T(8,128)S(1)} collective-permute-done((f32[2,16,1536]{2,1,0:T(8,128)}, f32[2,16,1536]{2,1,0:T(8,128)S(1)}, u32[]{:S(2)}, u32[]{:S(2)}) %collective-permute-start.20) | collective-permute-done | bytes 196640 | tf_op jit(solution)/shard_map/ppermute | solution.py:310
  131.9 3.8 %collective-permute-start.25 = (f32[2,16,1536]{2,1,0:T(8,128)}, f32[2,16,1536]{2,1,0:T(8,128)}, u32[]{:S(2)}, u32[]{:S(2)}) collective-permute-start(f32[2,16,1536]{2,1,0:T(8,128)} %get-tuple-element.67), channel_id=1, source_target_pairs={{0,26},{1,27},{2,24},{3,25},{4,30},{5,31},{6,28},{7,29},{8,18},{9,... | collective-permute-start | bytes 589832 | tf_op jit(solution)/shard_map/ppermute | solution.py:310
  135.7 2.5 collective-permute-done.21.refs_23_
  138.2 0.8 collective-permute-start.26
  139.0 10.7 %collective-permute-done.22.refs_24_ = f32[2,16,1536]{2,1,0:T(8,128)S(1)} collective-permute-done((f32[2,16,1536]{2,1,0:T(8,128)}, f32[2,16,1536]{2,1,0:T(8,128)S(1)}, u32[]{:S(2)}, u32[]{:S(2)}) %collective-permute-start.22) | collective-permute-done | bytes 196640 | tf_op jit(solution)/shard_map/ppermute | solution.py:310
  149.7 1.4 collective-permute-start.27
  151.2 3.6 %collective-permute-start.28 = (f32[2,16,1536]{2,1,0:T(8,128)}, f32[2,16,1536]{2,1,0:T(8,128)}, u32[]{:S(2)}, u32[]{:S(2)}) collective-permute-start(f32[2,16,1536]{2,1,0:T(8,128)} %get-tuple-element.70), channel_id=1, source_target_pairs={{0,29},{1,28},{2,31},{3,30},{4,25},{5,24},{6,27},{7,26},{8,21},{9,... | collective-permute-start | bytes 589832 | tf_op jit(solution)/shard_map/ppermute | solution.py:310
  154.7 3.0 collective-permute-start.29
  157.8 1.8 collective-permute-start.30
  160.2 5.3 %shard_map.64 = (f32[2,16,1536]{2,1,0:T(8,128)}, f32[2,16,1536]{2,1,0:T(8,128)}, f32[2,16,1536]{2,1,0:T(8,128)}, f32[2,16,1536]{2,1,0:T(8,128)}, f32[2,16,1536]{...) custom-call(s32[3]{0:T(128)} %get-tuple-element.77.refs_0_, s32[3]{0:T(128)} %refs_1_.9, ...), custom_call_target="tpu_custom_call" | custom-call | flops 50331648 | bytes 16777216 | tf_op jit(solution)/shard_map/pallas_call | solution.py:128
  165.6 5.4 %shard_map.65 = (f32[2,16,1536]{2,1,0:T(8,128)}, f32[2,16,1536]{2,1,0:T(8,128)}, f32[2,16,1536]{2,1,0:T(8,128)}, f32[2,16,1536]{2,1,0:T(8,128)}, f32[2,16,1536]{...) custom-call(s32[3]{0:T(128)} %get-tuple-element.78.refs_0_, s32[3]{0:T(128)} %refs_1_.9, ...), custom_call_target="tpu_custom_call" | custom-call | flops 50331648 | bytes 16777216 | tf_op jit(solution)/shard_map/pallas_call | solution.py:128
  171.0 1.0 collective-permute-start
  172.6 21.3 %collective-permute-start.10 = (f32[2,16,1536]{2,1,0:T(8,128)}, f32[2,16,1536]{2,1,0:T(8,128)S(1)}, u32[]{:S(2)}, u32[]{:S(2)}) collective-permute-start(f32[2,16,1536]{2,1,0:T(8,128)} %get-tuple-element.52), channel_id=1, source_target_pairs={{0,11},{1,10},{2,9},{3,8},{4,15},{5,14},{6,13},{7,12},{8,3},{9,2},... | collective-permute-start | bytes 589832 | tf_op jit(solution)/shard_map/ppermute | solution.py:310
  193.8 4.1 %collective-permute-start.11 = (f32[2,16,1536]{2,1,0:T(8,128)}, f32[2,16,1536]{2,1,0:T(8,128)S(1)}, u32[]{:S(2)}, u32[]{:S(2)}) collective-permute-start(f32[2,16,1536]{2,1,0:T(8,128)} %get-tuple-element.53), channel_id=1, source_target_pairs={{0,12},{1,13},{2,14},{3,15},{4,8},{5,9},{6,10},{7,11},{8,4},{9,5},... | collective-permute-start | bytes 589832 | tf_op jit(solution)/shard_map/ppermute | solution.py:310
  198.0 5.0 %collective-permute-start.12 = (f32[2,16,1536]{2,1,0:T(8,128)}, f32[2,16,1536]{2,1,0:T(8,128)S(1)}, u32[]{:S(2)}, u32[]{:S(2)}) collective-permute-start(f32[2,16,1536]{2,1,0:T(8,128)} %get-tuple-element.54), channel_id=1, source_target_pairs={{0,13},{1,12},{2,15},{3,14},{4,9},{5,8},{6,11},{7,10},{8,5},{9,4},... | collective-permute-start | bytes 589832 | tf_op jit(solution)/shard_map/ppermute | solution.py:310
  202.9 1.0 collective-permute-start.13
  204.0 5.5 %collective-permute-start.14 = (f32[2,16,1536]{2,1,0:T(8,128)}, f32[2,16,1536]{2,1,0:T(8,128)S(1)}, u32[]{:S(2)}, u32[]{:S(2)}) collective-permute-start(f32[2,16,1536]{2,1,0:T(8,128)} %get-tuple-element.56), channel_id=1, source_target_pairs={{0,15},{1,14},{2,13},{3,12},{4,11},{5,10},{6,9},{7,8},{8,7},{9,6},... | collective-permute-start | bytes 589832 | tf_op jit(solution)/shard_map/ppermute | solution.py:310
  209.5 1.6 collective-permute-start.2
  211.6 0.9 collective-permute-start.4
  212.5 2.4 collective-permute-done.13.refs_15_
  214.9 2.0 collective-permute-start.5
  216.8 2.2 collective-permute-done.14.refs_16_
  219.1 1.1 collective-permute-start.6
  220.2 1.4 collective-permute-done.2.refs_4_
  221.6 3.0 collective-permute-start.7
  224.7 6.4 %collective-permute-done.3.refs_5_ = f32[2,16,1536]{2,1,0:T(8,128)S(1)} collective-permute-done((f32[2,16,1536]{2,1,0:T(8,128)}, f32[2,16,1536]{2,1,0:T(8,128)S(1)}, u32[]{:S(2)}, u32[]{:S(2)}) %collective-permute-start.3) | collective-permute-done | bytes 196640 | tf_op jit(solution)/shard_map/ppermute | solution.py:310
  231.1 1.6 collective-permute-start.8
  232.7 2.4 collective-permute-done.4.refs_6_
  235.1 4.2 %collective-permute-start.9 = (f32[2,16,1536]{2,1,0:T(8,128)}, f32[2,16,1536]{2,1,0:T(8,128)S(1)}, u32[]{:S(2)}, u32[]{:S(2)}) collective-permute-start(f32[2,16,1536]{2,1,0:T(8,128)} %get-tuple-element.51), channel_id=1, source_target_pairs={{0,10},{1,11},{2,8},{3,9},{4,14},{5,15},{6,12},{7,13},{8,2},{9,3},... | collective-permute-start | bytes 589832 | tf_op jit(solution)/shard_map/ppermute | solution.py:310
  239.4 5.4 %collective-permute-done.9.refs_11_ = f32[2,16,1536]{2,1,0:T(8,128)S(1)} collective-permute-done((f32[2,16,1536]{2,1,0:T(8,128)}, f32[2,16,1536]{2,1,0:T(8,128)S(1)}, u32[]{:S(2)}, u32[]{:S(2)}) %collective-permute-start.9) | collective-permute-done | bytes 196640 | tf_op jit(solution)/shard_map/ppermute | solution.py:310
  245.5 24.2 %density_early.1 = (f32[512,1536]{1,0:T(8,128)}, bf16[1024,2048]{1,0:T(8,128)(2,1)}) custom-call(f32[2,512,512]{2,1,0:T(8,128)} %refs_0_.1, f32[2,16,1536]{2,1,0:T(8,128)} %get-tuple-element.41.refs_1_, f32[2,16,1536]{2,1,0:T(8,128)} %copy-done.8, f32[2,16,1536]{2,1,0:T(8,128)} %copy-done.9, f32[2,16,1536]{2,1,0:T(8,128)} %copy-done.18, ...), custom_call_target="tpu_custom_call" | custom-call | flops 15300820992 | bytes 16777216 | tf_op jit(solution)/shard_map/density_early/pallas_call | solution.py:248
  269.8 9.2 %density_late.1 = (f32[16,16,1024]{2,1,0:T(8,128)S(1)}, f32[16,16,1024]{2,1,0:T(8,128)S(1)}) custom-call(bf16[1024,2048]{1,0:T(8,128)(2,1)} %get-tuple-element.73.matrix_far, f32[32,2,16,512]{3,2,1,0:T(8,128)S(1)} %all-to-all-done.parts, f32[512,1536]{1,0:T(8,128)} %get-tuple-element.74.sums_far), custom_call_target="tpu_custom_call" | custom-call | flops 5100273664 | bytes 16777216 | tf_op jit(solution)/shard_map/density_late/pallas_call | solution.py:275
  279.0 2.6 collective-permute-done.31
  281.8 32.0 %all_to_all.10 = f32[16,16,1024]{2,1,0:T(8,128)S(1)} all-to-all(f32[16,16,1024]{2,1,0:T(8,128)S(1)} %add.3), channel_id=1, replica_groups={{0,2,4,6,8,10,12,14,16,18,20,22,24,26,28,30},{1,3,5,7,9,11,13,15,17,19,..., dimensions={0} | all-to-all | bytes 2097152 | tf_op jit(solution)/shard_map/all_to_all | solution.py:318
  313.9 0.7 reshape.8
  (84 shorter events, 4.4 us)
Async XLA Ops:
  8.1 261.6 %all-to-all-start = ((f32[32,2,16,512]{3,2,1,0:T(8,128)}), f32[32,2,16,512]{3,2,1,0:T(8,128)S(1)}, u32[]{:S(2)}, u32[]{:S(2)}) async-start(f32[32,2,16,512]{3,2,1,0:T(8,128)} %shard_map.68), calls=%async_computation | async-start | bytes 4194304 | tf_op jit(solution)/shard_map/all_to_all | solution.py:312
  21.6 68.6 %collective-permute-start.15 = (f32[2,16,1536]{2,1,0:T(8,128)}, f32[2,16,1536]{2,1,0:T(8,128)S(1)}, u32[]{:S(2)}, u32[]{:S(2)}) collective-permute-start(f32[2,16,1536]{2,1,0:T(8,128)} %get-tuple-element.57), channel_id=1, source_target_pairs={{0,16},{1,17},{2,18},{3,19},{4,20},{5,21},{6,22},{7,23},{8,24},{9,... | collective-permute-start | bytes 589832 | tf_op jit(solution)/shard_map/ppermute | solution.py:310
  24.1 73.4 %collective-permute-start.16 = (f32[2,16,1536]{2,1,0:T(8,128)}, f32[2,16,1536]{2,1,0:T(8,128)S(1)}, u32[]{:S(2)}, u32[]{:S(2)}) collective-permute-start(f32[2,16,1536]{2,1,0:T(8,128)} %get-tuple-element.58), channel_id=1, source_target_pairs={{0,17},{1,16},{2,19},{3,18},{4,21},{5,20},{6,23},{7,22},{8,25},{9,... | collective-permute-start | bytes 589832 | tf_op jit(solution)/shard_map/ppermute | solution.py:310
  24.1 88.0 %collective-permute-start.17 = (f32[2,16,1536]{2,1,0:T(8,128)}, f32[2,16,1536]{2,1,0:T(8,128)S(1)}, u32[]{:S(2)}, u32[]{:S(2)}) collective-permute-start(f32[2,16,1536]{2,1,0:T(8,128)} %get-tuple-element.59), channel_id=1, source_target_pairs={{0,18},{1,19},{2,16},{3,17},{4,22},{5,23},{6,20},{7,21},{8,26},{9,... | collective-permute-start | bytes 589832 | tf_op jit(solution)/shard_map/ppermute | solution.py:310
  27.3 87.8 %collective-permute-start.18 = (f32[2,16,1536]{2,1,0:T(8,128)}, f32[2,16,1536]{2,1,0:T(8,128)S(1)}, u32[]{:S(2)}, u32[]{:S(2)}) collective-permute-start(f32[2,16,1536]{2,1,0:T(8,128)} %get-tuple-element.60), channel_id=1, source_target_pairs={{0,19},{1,18},{2,17},{3,16},{4,23},{5,22},{6,21},{7,20},{8,27},{9,... | collective-permute-start | bytes 589832 | tf_op jit(solution)/shard_map/ppermute | solution.py:310
  27.7 92.6 %collective-permute-start.19 = (f32[2,16,1536]{2,1,0:T(8,128)}, f32[2,16,1536]{2,1,0:T(8,128)S(1)}, u32[]{:S(2)}, u32[]{:S(2)}) collective-permute-start(f32[2,16,1536]{2,1,0:T(8,128)} %get-tuple-element.61), channel_id=1, source_target_pairs={{0,20},{1,21},{2,22},{3,23},{4,16},{5,17},{6,18},{7,19},{8,28},{9,... | collective-permute-start | bytes 589832 | tf_op jit(solution)/shard_map/ppermute | solution.py:310
  90.2 41.7 %collective-permute-start.20 = (f32[2,16,1536]{2,1,0:T(8,128)}, f32[2,16,1536]{2,1,0:T(8,128)S(1)}, u32[]{:S(2)}, u32[]{:S(2)}) collective-permute-start(f32[2,16,1536]{2,1,0:T(8,128)} %get-tuple-element.62), channel_id=1, source_target_pairs={{0,21},{1,20},{2,23},{3,22},{4,17},{5,16},{6,19},{7,18},{8,29},{9,... | collective-permute-start | bytes 589832 | tf_op jit(solution)/shard_map/ppermute | solution.py:310
  97.4 68.1 %copy-start.1 = (f32[2,16,1536]{2,1,0:T(8,128)}, f32[2,16,1536]{2,1,0:T(8,128)S(1)}, u32[]{:S(2)}) copy-start(f32[2,16,1536]{2,1,0:T(8,128)S(1)} %collective-permute-done.16.refs_18_) | copy-start | bytes 589828
  97.4 40.8 %collective-permute-start.21 = (f32[2,16,1536]{2,1,0:T(8,128)}, f32[2,16,1536]{2,1,0:T(8,128)S(1)}, u32[]{:S(2)}, u32[]{:S(2)}) collective-permute-start(f32[2,16,1536]{2,1,0:T(8,128)} %get-tuple-element.63), channel_id=1, source_target_pairs={{0,22},{1,23},{2,20},{3,21},{4,18},{5,19},{6,16},{7,17},{8,30},{9,... | collective-permute-start | bytes 589832 | tf_op jit(solution)/shard_map/ppermute | solution.py:310
  112.0 53.4 %copy-start.2 = (f32[2,16,1536]{2,1,0:T(8,128)}, f32[2,16,1536]{2,1,0:T(8,128)S(1)}, u32[]{:S(2)}) copy-start(f32[2,16,1536]{2,1,0:T(8,128)S(1)} %collective-permute-done.17.refs_19_) | copy-start | bytes 589828
  112.0 37.7 %collective-permute-start.22 = (f32[2,16,1536]{2,1,0:T(8,128)}, f32[2,16,1536]{2,1,0:T(8,128)S(1)}, u32[]{:S(2)}, u32[]{:S(2)}) collective-permute-start(f32[2,16,1536]{2,1,0:T(8,128)} %get-tuple-element.64), channel_id=1, source_target_pairs={{0,23},{1,22},{2,21},{3,20},{4,19},{5,18},{6,17},{7,16},{8,31},{9,... | collective-permute-start | bytes 589832 | tf_op jit(solution)/shard_map/ppermute | solution.py:310
  115.1 50.4 %copy-start.3 = (f32[2,16,1536]{2,1,0:T(8,128)}, f32[2,16,1536]{2,1,0:T(8,128)S(1)}, u32[]{:S(2)}) copy-start(f32[2,16,1536]{2,1,0:T(8,128)S(1)} %collective-permute-done.18.refs_20_) | copy-start | bytes 589828
  115.1 36.0 %collective-permute-start.23 = (f32[2,16,1536]{2,1,0:T(8,128)}, f32[2,16,1536]{2,1,0:T(8,128)}, u32[]{:S(2)}, u32[]{:S(2)}) collective-permute-start(f32[2,16,1536]{2,1,0:T(8,128)} %get-tuple-element.65), channel_id=1, source_target_pairs={{0,24},{1,25},{2,26},{3,27},{4,28},{5,29},{6,30},{7,31},{8,16},{9,... | collective-permute-start | bytes 589832 | tf_op jit(solution)/shard_map/ppermute | solution.py:310
  120.4 45.1 %copy-start.4 = (f32[2,16,1536]{2,1,0:T(8,128)}, f32[2,16,1536]{2,1,0:T(8,128)S(1)}, u32[]{:S(2)}) copy-start(f32[2,16,1536]{2,1,0:T(8,128)S(1)} %collective-permute-done.19.refs_21_) | copy-start | bytes 589828
  120.4 34.4 %collective-permute-start.24 = (f32[2,16,1536]{2,1,0:T(8,128)}, f32[2,16,1536]{2,1,0:T(8,128)}, u32[]{:S(2)}, u32[]{:S(2)}) collective-permute-start(f32[2,16,1536]{2,1,0:T(8,128)} %get-tuple-element.66), channel_id=1, source_target_pairs={{0,25},{1,24},{2,27},{3,26},{4,29},{5,28},{6,31},{7,30},{8,17},{9,... | collective-permute-start | bytes 589832 | tf_op jit(solution)/shard_map/ppermute | solution.py:310
  131.9 33.6 %copy-start.5 = (f32[2,16,1536]{2,1,0:T(8,128)}, f32[2,16,1536]{2,1,0:T(8,128)S(1)}, u32[]{:S(2)}) copy-start(f32[2,16,1536]{2,1,0:T(8,128)S(1)} %collective-permute-done.20.refs_22_) | copy-start | bytes 589828
  131.9 25.9 %collective-permute-start.25 = (f32[2,16,1536]{2,1,0:T(8,128)}, f32[2,16,1536]{2,1,0:T(8,128)}, u32[]{:S(2)}, u32[]{:S(2)}) collective-permute-start(f32[2,16,1536]{2,1,0:T(8,128)} %get-tuple-element.67), channel_id=1, source_target_pairs={{0,26},{1,27},{2,24},{3,25},{4,30},{5,31},{6,28},{7,29},{8,18},{9,... | collective-permute-start | bytes 589832 | tf_op jit(solution)/shard_map/ppermute | solution.py:310
  138.2 27.3 %copy-start.6 = (f32[2,16,1536]{2,1,0:T(8,128)}, f32[2,16,1536]{2,1,0:T(8,128)S(1)}, u32[]{:S(2)}) copy-start(f32[2,16,1536]{2,1,0:T(8,128)S(1)} %collective-permute-done.21.refs_23_) | copy-start | bytes 589828
  138.2 32.8 %collective-permute-start.26 = (f32[2,16,1536]{2,1,0:T(8,128)}, f32[2,16,1536]{2,1,0:T(8,128)}, u32[]{:S(2)}, u32[]{:S(2)}) collective-permute-start(f32[2,16,1536]{2,1,0:T(8,128)} %get-tuple-element.68), channel_id=1, source_target_pairs={{0,27},{1,26},{2,25},{3,24},{4,31},{5,30},{6,29},{7,28},{8,19},{9,... | collective-permute-start | bytes 589832 | tf_op jit(solution)/shard_map/ppermute | solution.py:310
  149.7 22.3 %collective-permute-start.27 = (f32[2,16,1536]{2,1,0:T(8,128)}, f32[2,16,1536]{2,1,0:T(8,128)}, u32[]{:S(2)}, u32[]{:S(2)}) collective-permute-start(f32[2,16,1536]{2,1,0:T(8,128)} %get-tuple-element.69), channel_id=1, source_target_pairs={{0,28},{1,29},{2,30},{3,31},{4,24},{5,25},{6,26},{7,27},{8,20},{9,... | collective-permute-start | bytes 589832 | tf_op jit(solution)/shard_map/ppermute | solution.py:310
  151.2 21.4 %collective-permute-start.28 = (f32[2,16,1536]{2,1,0:T(8,128)}, f32[2,16,1536]{2,1,0:T(8,128)}, u32[]{:S(2)}, u32[]{:S(2)}) collective-permute-start(f32[2,16,1536]{2,1,0:T(8,128)} %get-tuple-element.70), channel_id=1, source_target_pairs={{0,29},{1,28},{2,31},{3,30},{4,25},{5,24},{6,27},{7,26},{8,21},{9,... | collective-permute-start | bytes 589832 | tf_op jit(solution)/shard_map/ppermute | solution.py:310
  154.7 39.1 %collective-permute-start.29 = (f32[2,16,1536]{2,1,0:T(8,128)}, f32[2,16,1536]{2,1,0:T(8,128)}, u32[]{:S(2)}, u32[]{:S(2)}) collective-permute-start(f32[2,16,1536]{2,1,0:T(8,128)} %get-tuple-element.71), channel_id=1, source_target_pairs={{0,30},{1,31},{2,28},{3,29},{4,26},{5,27},{6,24},{7,25},{8,22},{9,... | collective-permute-start | bytes 589832 | tf_op jit(solution)/shard_map/ppermute | solution.py:310
  157.8 40.2 %collective-permute-start.30 = (f32[2,16,1536]{2,1,0:T(8,128)}, f32[2,16,1536]{2,1,0:T(8,128)}, u32[]{:S(2)}, u32[]{:S(2)}) collective-permute-start(f32[2,16,1536]{2,1,0:T(8,128)} %get-tuple-element.72), channel_id=1, source_target_pairs={{0,31},{1,30},{2,29},{3,28},{4,27},{5,26},{6,25},{7,24},{8,23},{9,... | collective-permute-start | bytes 589832 | tf_op jit(solution)/shard_map/ppermute | solution.py:310
  165.5 46.1 %copy-start.14 = (f32[2,16,1536]{2,1,0:T(8,128)S(1)}, f32[2,16,1536]{2,1,0:T(8,128)}, u32[]{:S(2)}) copy-start(f32[2,16,1536]{2,1,0:T(8,128)} %get-tuple-element.46) | copy-start | bytes 589828
  165.6 49.3 %copy-start.12 = (f32[2,16,1536]{2,1,0:T(8,128)S(1)}, f32[2,16,1536]{2,1,0:T(8,128)}, u32[]{:S(2)}) copy-start(f32[2,16,1536]{2,1,0:T(8,128)} %get-tuple-element.47) | copy-start | bytes 589828
  165.6 53.5 %copy-start.11 = (f32[2,16,1536]{2,1,0:T(8,128)S(1)}, f32[2,16,1536]{2,1,0:T(8,128)}, u32[]{:S(2)}) copy-start(f32[2,16,1536]{2,1,0:T(8,128)} %get-tuple-element.48) | copy-start | bytes 589828
  171.0 31.9 %collective-permute-start = (f32[2,16,1536]{2,1,0:T(8,128)}, f32[2,16,1536]{2,1,0:T(8,128)S(1)}, u32[]{:S(2)}, u32[]{:S(2)}) collective-permute-start(f32[2,16,1536]{2,1,0:T(8,128)} %get-tuple-element.42), channel_id=1, source_target_pairs={{0,1},{1,0},{2,3},{3,2},{4,5},{5,4},{6,7},{7,6},{8,9},{9,8},{10,11... | collective-permute-start | bytes 589832 | tf_op jit(solution)/shard_map/ppermute | solution.py:310
  172.0 32.0 %collective-permute-start.1 = (f32[2,16,1536]{2,1,0:T(8,128)}, f32[2,16,1536]{2,1,0:T(8,128)S(1)}, u32[]{:S(2)}, u32[]{:S(2)}) collective-permute-start(f32[2,16,1536]{2,1,0:T(8,128)} %get-tuple-element.43), channel_id=1, source_target_pairs={{0,2},{1,3},{2,0},{3,1},{4,6},{5,7},{6,4},{7,5},{8,10},{9,11},{10,... | collective-permute-start | bytes 589832 | tf_op jit(solution)/shard_map/ppermute | solution.py:310
  172.6 36.9 %collective-permute-start.10 = (f32[2,16,1536]{2,1,0:T(8,128)}, f32[2,16,1536]{2,1,0:T(8,128)S(1)}, u32[]{:S(2)}, u32[]{:S(2)}) collective-permute-start(f32[2,16,1536]{2,1,0:T(8,128)} %get-tuple-element.52), channel_id=1, source_target_pairs={{0,11},{1,10},{2,9},{3,8},{4,15},{5,14},{6,13},{7,12},{8,3},{9,2},... | collective-permute-start | bytes 589832 | tf_op jit(solution)/shard_map/ppermute | solution.py:310
  193.8 17.2 %collective-permute-start.11 = (f32[2,16,1536]{2,1,0:T(8,128)}, f32[2,16,1536]{2,1,0:T(8,128)S(1)}, u32[]{:S(2)}, u32[]{:S(2)}) collective-permute-start(f32[2,16,1536]{2,1,0:T(8,128)} %get-tuple-element.53), channel_id=1, source_target_pairs={{0,12},{1,13},{2,14},{3,15},{4,8},{5,9},{6,10},{7,11},{8,4},{9,5},... | collective-permute-start | bytes 589832 | tf_op jit(solution)/shard_map/ppermute | solution.py:310
  198.0 13.6 %collective-permute-start.12 = (f32[2,16,1536]{2,1,0:T(8,128)}, f32[2,16,1536]{2,1,0:T(8,128)S(1)}, u32[]{:S(2)}, u32[]{:S(2)}) collective-permute-start(f32[2,16,1536]{2,1,0:T(8,128)} %get-tuple-element.54), channel_id=1, source_target_pairs={{0,13},{1,12},{2,15},{3,14},{4,9},{5,8},{6,11},{7,10},{8,5},{9,4},... | collective-permute-start | bytes 589832 | tf_op jit(solution)/shard_map/ppermute | solution.py:310
  202.9 41.9 %copy-start.8 = (f32[2,16,1536]{2,1,0:T(8,128)}, f32[2,16,1536]{2,1,0:T(8,128)S(1)}, u32[]{:S(2)}) copy-start(f32[2,16,1536]{2,1,0:T(8,128)S(1)} %collective-permute-done.refs_2_) | copy-start | bytes 589828
  202.9 11.9 %collective-permute-start.13 = (f32[2,16,1536]{2,1,0:T(8,128)}, f32[2,16,1536]{2,1,0:T(8,128)S(1)}, u32[]{:S(2)}, u32[]{:S(2)}) collective-permute-start(f32[2,16,1536]{2,1,0:T(8,128)} %get-tuple-element.55), channel_id=1, source_target_pairs={{0,14},{1,15},{2,12},{3,13},{4,10},{5,11},{6,8},{7,9},{8,6},{9,7},... | collective-permute-start | bytes 589832 | tf_op jit(solution)/shard_map/ppermute | solution.py:310
  204.0 40.9 %copy-start.9 = (f32[2,16,1536]{2,1,0:T(8,128)}, f32[2,16,1536]{2,1,0:T(8,128)S(1)}, u32[]{:S(2)}) copy-start(f32[2,16,1536]{2,1,0:T(8,128)S(1)} %collective-permute-done.1.refs_3_) | copy-start | bytes 589828
  204.0 15.1 %collective-permute-start.14 = (f32[2,16,1536]{2,1,0:T(8,128)}, f32[2,16,1536]{2,1,0:T(8,128)S(1)}, u32[]{:S(2)}, u32[]{:S(2)}) collective-permute-start(f32[2,16,1536]{2,1,0:T(8,128)} %get-tuple-element.56), channel_id=1, source_target_pairs={{0,15},{1,14},{2,13},{3,12},{4,11},{5,10},{6,9},{7,8},{8,7},{9,6},... | collective-permute-start | bytes 589832 | tf_op jit(solution)/shard_map/ppermute | solution.py:310
  209.5 35.4 %copy-start.10 = (f32[2,16,1536]{2,1,0:T(8,128)}, f32[2,16,1536]{2,1,0:T(8,128)S(1)}, u32[]{:S(2)}) copy-start(f32[2,16,1536]{2,1,0:T(8,128)S(1)} %collective-permute-done.10.refs_12_) | copy-start | bytes 589828
  209.5 12.2 %collective-permute-start.2 = (f32[2,16,1536]{2,1,0:T(8,128)}, f32[2,16,1536]{2,1,0:T(8,128)S(1)}, u32[]{:S(2)}, u32[]{:S(2)}) collective-permute-start(f32[2,16,1536]{2,1,0:T(8,128)} %get-tuple-element.44), channel_id=1, source_target_pairs={{0,3},{1,2},{2,1},{3,0},{4,7},{5,6},{6,5},{7,4},{8,11},{9,10},{10,... | collective-permute-start | bytes 589832 | tf_op jit(solution)/shard_map/ppermute | solution.py:310
  211.0 33.8 %copy-start.13 = (f32[2,16,1536]{2,1,0:T(8,128)}, f32[2,16,1536]{2,1,0:T(8,128)S(1)}, u32[]{:S(2)}) copy-start(f32[2,16,1536]{2,1,0:T(8,128)S(1)} %collective-permute-done.11.refs_13_) | copy-start | bytes 589828
  211.0 20.0 %collective-permute-start.3 = (f32[2,16,1536]{2,1,0:T(8,128)}, f32[2,16,1536]{2,1,0:T(8,128)S(1)}, u32[]{:S(2)}, u32[]{:S(2)}) collective-permute-start(f32[2,16,1536]{2,1,0:T(8,128)} %get-tuple-element.45), channel_id=1, source_target_pairs={{0,4},{1,5},{2,6},{3,7},{4,0},{5,1},{6,2},{7,3},{8,12},{9,13},{10,... | collective-permute-start | bytes 589832 | tf_op jit(solution)/shard_map/ppermute | solution.py:310
  211.6 27.7 %copy-start.15 = (f32[2,16,1536]{2,1,0:T(8,128)}, f32[2,16,1536]{2,1,0:T(8,128)S(1)}, u32[]{:S(2)}) copy-start(f32[2,16,1536]{2,1,0:T(8,128)S(1)} %collective-permute-done.12.refs_14_) | copy-start | bytes 589828
  211.6 23.5 %collective-permute-start.4 = (f32[2,16,1536]{2,1,0:T(8,128)S(1)}, f32[2,16,1536]{2,1,0:T(8,128)S(1)}, u32[]{:S(2)}, u32[]{:S(2)}) collective-permute-start(f32[2,16,1536]{2,1,0:T(8,128)S(1)} %copy-done.14), channel_id=1, source_target_pairs={{0,5},{1,4},{2,7},{3,6},{4,1},{5,0},{6,3},{7,2},{8,13},{9,12},{10,... | collective-permute-start | bytes 589832 | tf_op jit(solution)/shard_map/ppermute | solution.py:310
  214.9 24.5 %copy-start.16 = (f32[2,16,1536]{2,1,0:T(8,128)}, f32[2,16,1536]{2,1,0:T(8,128)S(1)}, u32[]{:S(2)}) copy-start(f32[2,16,1536]{2,1,0:T(8,128)S(1)} %collective-permute-done.13.refs_15_) | copy-start | bytes 589828
  214.9 24.5 %collective-permute-start.5 = (f32[2,16,1536]{2,1,0:T(8,128)S(1)}, f32[2,16,1536]{2,1,0:T(8,128)S(1)}, u32[]{:S(2)}, u32[]{:S(2)}) collective-permute-start(f32[2,16,1536]{2,1,0:T(8,128)S(1)} %copy-done.12), channel_id=1, source_target_pairs={{0,6},{1,7},{2,4},{3,5},{4,2},{5,3},{6,0},{7,1},{8,14},{9,15},{10,... | collective-permute-start | bytes 589832 | tf_op jit(solution)/shard_map/ppermute | solution.py:310
  219.1 20.3 %collective-permute-start.6 = (f32[2,16,1536]{2,1,0:T(8,128)S(1)}, f32[2,16,1536]{2,1,0:T(8,128)S(1)}, u32[]{:S(2)}, u32[]{:S(2)}) collective-permute-start(f32[2,16,1536]{2,1,0:T(8,128)S(1)} %copy-done.11), channel_id=1, source_target_pairs={{0,7},{1,6},{2,5},{3,4},{4,3},{5,2},{6,1},{7,0},{8,15},{9,14},{10,... | collective-permute-start | bytes 589832 | tf_op jit(solution)/shard_map/ppermute | solution.py:310
  221.6 17.7 %collective-permute-start.7 = (f32[2,16,1536]{2,1,0:T(8,128)}, f32[2,16,1536]{2,1,0:T(8,128)S(1)}, u32[]{:S(2)}, u32[]{:S(2)}) collective-permute-start(f32[2,16,1536]{2,1,0:T(8,128)} %get-tuple-element.49), channel_id=1, source_target_pairs={{0,8},{1,9},{2,10},{3,11},{4,12},{5,13},{6,14},{7,15},{8,0},{9,1},... | collective-permute-start | bytes 589832 | tf_op jit(solution)/shard_map/ppermute | solution.py:310
  231.1 8.3 %collective-permute-start.8 = (f32[2,16,1536]{2,1,0:T(8,128)}, f32[2,16,1536]{2,1,0:T(8,128)S(1)}, u32[]{:S(2)}, u32[]{:S(2)}) collective-permute-start(f32[2,16,1536]{2,1,0:T(8,128)} %get-tuple-element.50), channel_id=1, source_target_pairs={{0,9},{1,8},{2,11},{3,10},{4,13},{5,12},{6,15},{7,14},{8,1},{9,0},... | collective-permute-start | bytes 589832 | tf_op jit(solution)/shard_map/ppermute | solution.py:310
  235.1 9.7 %collective-permute-start.9 = (f32[2,16,1536]{2,1,0:T(8,128)}, f32[2,16,1536]{2,1,0:T(8,128)S(1)}, u32[]{:S(2)}, u32[]{:S(2)}) collective-permute-start(f32[2,16,1536]{2,1,0:T(8,128)} %get-tuple-element.51), channel_id=1, source_target_pairs={{0,10},{1,11},{2,8},{3,9},{4,14},{5,15},{6,12},{7,13},{8,2},{9,3},... | collective-permute-start | bytes 589832 | tf_op jit(solution)/shard_map/ppermute | solution.py:310
  278.9 2.7 collective-permute-start.31
  (11 other events, 110.4 us)

commit v3 on v2

--- a/solution.py
+++ b/solution.py
@@ -225,13 +225,16 @@
     cross = sums[:, 2 * width :]
     sums[:, :width] = sums[:, :width] + mixed + mixed.T
     sums[:, width : 2 * width] = cross - cross.T
-    parity = lax.rem(lax.axis_index("cfg"), 2)
-    own = keep.shape[1]
-    for chip in range(keep.shape[0]):
-        near = pl.multiple_of((2 * chip + parity) * own, own)
-        far = pl.multiple_of((2 * chip + 1 - parity) * own, own)
-        keep[chip] = sums[pl.ds(near, own), pl.ds(0, 2 * width)]
-        send[chip] = sums[pl.ds(far, own), pl.ds(0, 2 * width)]
+    me = lax.axis_index("cfg")
+    chip, core = jnp.right_shift(me, 1), me & 1
+    inner, planes, own, _ = keep.shape
+    for near in range(inner):
+        for plane in range(planes):
+            target = 2 * (chip ^ (plane * inner + near))
+            mine = pl.ds(pl.multiple_of((target + core) * own, own), own)
+            other = pl.ds(pl.multiple_of((target + 1 - core) * own, own), own)
+            keep[near, plane] = sums[mine, pl.ds(0, 2 * width)]
+            send[near, plane] = sums[other, pl.ds(0, 2 * width)]
 
 
 def cost(slots, width, n):
@@ -271,7 +274,7 @@
 def density_late(matrix, parts, sums, devices):
     n = matrix.shape[0] // 2
     width = sums.shape[0]
-    half = jax.ShapeDtypeStruct((devices // 2, width // devices, 2 * width), jnp.float32)
+    half = jax.ShapeDtypeStruct((devices // 8, 4, width // devices, 2 * width), jnp.float32)
     return pl.pallas_call(
         density_late_body,
         in_specs=[far, vmem, far],
@@ -312,11 +315,28 @@
     parts = lax.all_to_all(packed, "cfg", split_axis=0, concat_axis=0, tiled=True)
     sums, matrix = density_early(prop_third, arrived, width)
     keep, send = density_late(matrix, parts, sums, devices)
-    swap = [(i, i ^ 1) for i in range(devices)]
-    half = keep + lax.ppermute(send, "cfg", swap)
-    groups = [list(range(core, devices, 2)) for core in range(2)]
-    pieces = lax.all_to_all(half, "cfg", split_axis=0, concat_axis=0, tiled=True, axis_index_groups=groups)
-    return jnp.sum(pieces, axis=0).reshape(-1, 2, width)
+    return reduce_sums(keep, send, devices)
+
+
+def passed(values, distance, devices):
+    return lax.ppermute(values, "cfg", [(i, i ^ distance) for i in range(devices)])
+
+
+def reduce_sums(keep, send, devices):
+    inner, planes, own, lanes = keep.shape
+    other = passed(send, 1, devices)
+    near = [keep[k] + other[k] for k in range(inner)]
+    arrived = [passed(near[k], 2 * k, devices) for k in range(inner - 1, 0, -1)]
+    blocks = []
+    for plane in range(planes):
+        block = near[0][plane]
+        for values in arrived:
+            block = block + values[plane]
+        blocks.append(block)
+    total = blocks[0]
+    for values in [passed(blocks[plane], 2 * inner * plane, devices) for plane in range(planes - 1, 0, -1)]:
+        total = total + values
+    return total.reshape(own, 2, lanes // 2)
 
 
 def boundary_terms(first, second, third, detune_steps):
@@ -398,7 +418,7 @@
         rows = amplitudes.shape[1]
         seconds, width = amplitudes.shape[2:]
         powers = devices & (devices - 1) == 0
-        if rows % 16 or seconds != tile or seconds // devices < 2 or (width // devices) % 8 or width % tile or not powers:
+        if rows % 16 or devices % 8 or seconds != tile or seconds // devices < 2 or (width // devices) % 8 or width % tile or not powers:
             return plain_shards(amplitudes, *others)
         return shards(amplitudes, *others, devices)
 

time: 315 us -> 307 us (0.975)
  blocking collectives: 32 us -> 0 us
  waiting for transfers between devices: 129 us -> 146 us
  starting transfers between devices: 87.5 us -> 95.5 us
    all_to_all x1 -> x0, blocking collectives: 32 us -> none  [shards(): lax.all_to_all(half, 'cfg', split_axis=0, concat_axis=0, tiled=True, axis...]
    ppermute x1 -> x7, waiting for transfers between devices: 2.65 us -> 19.4 us  [passed(): lax.ppermute(values, 'cfg', [(i, i ^ distance) for i in range(devices)])]
    ppermute x1 -> x7, starting transfers between devices: 0.07 us -> 8.08 us  [passed(): lax.ppermute(values, 'cfg', [(i, i ^ distance) for i in range(devices)])]
  transfers between devices with their start and end apart: 33 -> 39, of which waited for: 15 -> 19; matrix products, arithmetic and copies ran while one was open for 0% -> 0% of each run, Pallas kernels for 14% -> 15%
where the time goes in v3:
time: 307 us
  waiting for transfers between devices  146 us (48%)
  starting transfers between devices  95.5 us (31%)
  Pallas kernels  61.6 us (20%)
    ppermute x31, waiting for transfers between devices, shards(): arrived[distance] = lax.ppermute(blocks[distance], 'cfg', pairs)  127 us
    ppermute x31, starting transfers between devices, shards(): arrived[distance] = lax.ppermute(blocks[distance], 'cfg', pairs)  79.9 us
    pallas_call x5, Pallas kernels, pack(): pl.pallas_call(lambda *refs: pack_body(shape, first_slot, group, *refs),...  28.8 us
    pallas_call x1, Pallas kernels, density_early(): pl.pallas_call(lambda *refs: density_early_body(len(parts), *refs), grid=...  24.2 us
    ppermute x7, waiting for transfers between devices, passed(): lax.ppermute(values, 'cfg', [(i, i ^ distance) for i in range(devices)])  19.4 us
    pallas_call x1, Pallas kernels, density_late(): pl.pallas_call(density_late_body, in_specs=[far, vmem, far], out_specs=(v...  8.58 us
    ppermute x7, starting transfers between devices, passed(): lax.ppermute(values, 'cfg', [(i, i ^ distance) for i in range(devices)])  8.08 us
    all_to_all x1, starting transfers between devices, shards(): lax.all_to_all(packed, 'cfg', split_axis=0, concat_axis=0, tiled=True)  7.51 us
  transfers between devices with their start and end apart: 39, of which 19 were waited for; matrix products, arithmetic and copies ran while one was open for 0% of the time, Pallas kernels for 15%

profile of v3, /device:TPU:0, one launch (start us, length us, event | category | flops | bytes accessed | tf_op | source)
XLA Modules:
  0.0 306.7 jit_solution(10340330639600406942)
XLA Ops:
  0.5 7.6 %shard_map.68 = f32[32,2,16,512]{3,2,1,0:T(8,128)} custom-call(s32[3]{0:T(128)} %broadcast_1_refs_0_.2.refs_0_, s32[3]{0:T(128)} %refs_1_.9, s32[16]{0:T(128)} %refs_2_.9, s32[128]{0:T(128)} %refs_3_.9, s32[1,512]{1,0:T(1,128)} %bitcast.46, s32[1,128]{1,0:T(1,128)} %bitcast.51, f32[2,16,128,512]{3,2,1,0:T(8,128)} %refs_9_.9, f32[2,16,128,512]{3,2,1,0:T(8,128)} %refs_9_.9, ...), custom_call_target="tpu_custom_call" | custom-call | flops 50331648 | bytes 16777216 | tf_op jit(solution)/shard_map/pallas_call | solution.py:128
  8.1 7.5 %all-to-all-start = ((f32[32,2,16,512]{3,2,1,0:T(8,128)}), f32[32,2,16,512]{3,2,1,0:T(8,128)S(1)}, u32[]{:S(2)}, u32[]{:S(2)}) async-start(f32[32,2,16,512]{3,2,1,0:T(8,128)} %shard_map.68), calls=%async_computation | async-start | bytes 4194304 | tf_op jit(solution)/shard_map/all_to_all | solution.py:315
  16.3 5.3 %shard_map.66 = (f32[2,16,1536]{2,1,0:T(8,128)}, f32[2,16,1536]{2,1,0:T(8,128)}, f32[2,16,1536]{2,1,0:T(8,128)}, f32[2,16,1536]{2,1,0:T(8,128)}, f32[2,16,1536]{...) custom-call(s32[3]{0:T(128)} %get-tuple-element.86.refs_0_, s32[3]{0:T(128)} %refs_1_.9, ...), custom_call_target="tpu_custom_call" | custom-call | flops 50331648 | bytes 16777216 | tf_op jit(solution)/shard_map/pallas_call | solution.py:128
  21.5 2.5 collective-permute-start.15
  24.0 3.3 %collective-permute-start.17 = (f32[2,16,1536]{2,1,0:T(8,128)}, f32[2,16,1536]{2,1,0:T(8,128)S(1)}, u32[]{:S(2)}, u32[]{:S(2)}) collective-permute-start(f32[2,16,1536]{2,1,0:T(8,128)} %get-tuple-element.59), channel_id=1, source_target_pairs={{0,18},{1,19},{2,16},{3,17},{4,22},{5,23},{6,20},{7,21},{8,26},{9,... | collective-permute-start | bytes 589832 | tf_op jit(solution)/shard_map/ppermute | solution.py:313
  27.7 3.4 %collective-permute-start.19 = (f32[2,16,1536]{2,1,0:T(8,128)}, f32[2,16,1536]{2,1,0:T(8,128)S(1)}, u32[]{:S(2)}, u32[]{:S(2)}) collective-permute-start(f32[2,16,1536]{2,1,0:T(8,128)} %get-tuple-element.61), channel_id=1, source_target_pairs={{0,20},{1,21},{2,22},{3,23},{4,16},{5,17},{6,18},{7,19},{8,28},{9,... | collective-permute-start | bytes 589832 | tf_op jit(solution)/shard_map/ppermute | solution.py:313
  31.1 59.0 %collective-permute-done.15.refs_17_ = f32[2,16,1536]{2,1,0:T(8,128)S(1)} collective-permute-done((f32[2,16,1536]{2,1,0:T(8,128)}, f32[2,16,1536]{2,1,0:T(8,128)S(1)}, u32[]{:S(2)}, u32[]{:S(2)}) %collective-permute-start.15) | collective-permute-done | bytes 196640 | tf_op jit(solution)/shard_map/ppermute | solution.py:313
  90.2 5.3 %shard_map.67 = (f32[2,16,1536]{2,1,0:T(8,128)}, f32[2,16,1536]{2,1,0:T(8,128)}, f32[2,16,1536]{2,1,0:T(8,128)}, f32[2,16,1536]{2,1,0:T(8,128)}, f32[2,16,1536]{...) custom-call(s32[3]{0:T(128)} %get-tuple-element.87.refs_0_, s32[3]{0:T(128)} %refs_1_.9, ...), custom_call_target="tpu_custom_call" | custom-call | flops 50331648 | bytes 16777216 | tf_op jit(solution)/shard_map/pallas_call | solution.py:128
  95.5 2.0 collective-permute-done.16.refs_18_
  97.4 2.5 collective-permute-start.21
  100.0 12.1 %collective-permute-done.17.refs_19_ = f32[2,16,1536]{2,1,0:T(8,128)S(1)} collective-permute-done((f32[2,16,1536]{2,1,0:T(8,128)}, f32[2,16,1536]{2,1,0:T(8,128)S(1)}, u32[]{:S(2)}, u32[]{:S(2)}) %collective-permute-start.17) | collective-permute-done | bytes 196640 | tf_op jit(solution)/shard_map/ppermute | solution.py:313
  112.0 3.1 %collective-permute-done.18.refs_20_ = f32[2,16,1536]{2,1,0:T(8,128)S(1)} collective-permute-done((f32[2,16,1536]{2,1,0:T(8,128)}, f32[2,16,1536]{2,1,0:T(8,128)S(1)}, u32[]{:S(2)}, u32[]{:S(2)}) %collective-permute-start.18) | collective-permute-done | bytes 196640 | tf_op jit(solution)/shard_map/ppermute | solution.py:313
  115.1 5.2 %collective-permute-done.19.refs_21_ = f32[2,16,1536]{2,1,0:T(8,128)S(1)} collective-permute-done((f32[2,16,1536]{2,1,0:T(8,128)}, f32[2,16,1536]{2,1,0:T(8,128)S(1)}, u32[]{:S(2)}, u32[]{:S(2)}) %collective-permute-start.19) | collective-permute-done | bytes 196640 | tf_op jit(solution)/shard_map/ppermute | solution.py:313
  120.4 11.5 %collective-permute-done.20.refs_22_ = f32[2,16,1536]{2,1,0:T(8,128)S(1)} collective-permute-done((f32[2,16,1536]{2,1,0:T(8,128)}, f32[2,16,1536]{2,1,0:T(8,128)S(1)}, u32[]{:S(2)}, u32[]{:S(2)}) %collective-permute-start.20) | collective-permute-done | bytes 196640 | tf_op jit(solution)/shard_map/ppermute | solution.py:313
  131.9 3.8 %collective-permute-start.25 = (f32[2,16,1536]{2,1,0:T(8,128)}, f32[2,16,1536]{2,1,0:T(8,128)}, u32[]{:S(2)}, u32[]{:S(2)}) collective-permute-start(f32[2,16,1536]{2,1,0:T(8,128)} %get-tuple-element.67), channel_id=1, source_target_pairs={{0,26},{1,27},{2,24},{3,25},{4,30},{5,31},{6,28},{7,29},{8,18},{9,... | collective-permute-start | bytes 589832 | tf_op jit(solution)/shard_map/ppermute | solution.py:313
  135.7 2.5 collective-permute-done.21.refs_23_
  139.0 10.7 %collective-permute-done.22.refs_24_ = f32[2,16,1536]{2,1,0:T(8,128)S(1)} collective-permute-done((f32[2,16,1536]{2,1,0:T(8,128)}, f32[2,16,1536]{2,1,0:T(8,128)S(1)}, u32[]{:S(2)}, u32[]{:S(2)}) %collective-permute-start.22) | collective-permute-done | bytes 196640 | tf_op jit(solution)/shard_map/ppermute | solution.py:313
  149.7 1.4 collective-permute-start.27
  151.2 3.6 %collective-permute-start.28 = (f32[2,16,1536]{2,1,0:T(8,128)}, f32[2,16,1536]{2,1,0:T(8,128)}, u32[]{:S(2)}, u32[]{:S(2)}) collective-permute-start(f32[2,16,1536]{2,1,0:T(8,128)} %get-tuple-element.70), channel_id=1, source_target_pairs={{0,29},{1,28},{2,31},{3,30},{4,25},{5,24},{6,27},{7,26},{8,21},{9,... | collective-permute-start | bytes 589832 | tf_op jit(solution)/shard_map/ppermute | solution.py:313
  154.7 3.0 collective-permute-start.29
  157.8 1.8 collective-permute-start.30
  160.1 5.2 %shard_map.64 = (f32[2,16,1536]{2,1,0:T(8,128)}, f32[2,16,1536]{2,1,0:T(8,128)}, f32[2,16,1536]{2,1,0:T(8,128)}, f32[2,16,1536]{2,1,0:T(8,128)}, f32[2,16,1536]{...) custom-call(s32[3]{0:T(128)} %get-tuple-element.84.refs_0_, s32[3]{0:T(128)} %refs_1_.9, ...), custom_call_target="tpu_custom_call" | custom-call | flops 50331648 | bytes 16777216 | tf_op jit(solution)/shard_map/pallas_call | solution.py:128
  165.5 5.4 %shard_map.65 = (f32[2,16,1536]{2,1,0:T(8,128)}, f32[2,16,1536]{2,1,0:T(8,128)}, f32[2,16,1536]{2,1,0:T(8,128)}, f32[2,16,1536]{2,1,0:T(8,128)}, f32[2,16,1536]{...) custom-call(s32[3]{0:T(128)} %get-tuple-element.85.refs_0_, s32[3]{0:T(128)} %refs_1_.9, ...), custom_call_target="tpu_custom_call" | custom-call | flops 50331648 | bytes 16777216 | tf_op jit(solution)/shard_map/pallas_call | solution.py:128
  172.5 21.3 %collective-permute-start.10 = (f32[2,16,1536]{2,1,0:T(8,128)}, f32[2,16,1536]{2,1,0:T(8,128)S(1)}, u32[]{:S(2)}, u32[]{:S(2)}) collective-permute-start(f32[2,16,1536]{2,1,0:T(8,128)} %get-tuple-element.52), channel_id=1, source_target_pairs={{0,11},{1,10},{2,9},{3,8},{4,15},{5,14},{6,13},{7,12},{8,3},{9,2},... | collective-permute-start | bytes 589832 | tf_op jit(solution)/shard_map/ppermute | solution.py:313
  193.8 4.2 %collective-permute-start.11 = (f32[2,16,1536]{2,1,0:T(8,128)}, f32[2,16,1536]{2,1,0:T(8,128)S(1)}, u32[]{:S(2)}, u32[]{:S(2)}) collective-permute-start(f32[2,16,1536]{2,1,0:T(8,128)} %get-tuple-element.53), channel_id=1, source_target_pairs={{0,12},{1,13},{2,14},{3,15},{4,8},{5,9},{6,10},{7,11},{8,4},{9,5},... | collective-permute-start | bytes 589832 | tf_op jit(solution)/shard_map/ppermute | solution.py:313
  198.0 5.0 %collective-permute-start.12 = (f32[2,16,1536]{2,1,0:T(8,128)}, f32[2,16,1536]{2,1,0:T(8,128)S(1)}, u32[]{:S(2)}, u32[]{:S(2)}) collective-permute-start(f32[2,16,1536]{2,1,0:T(8,128)} %get-tuple-element.54), channel_id=1, source_target_pairs={{0,13},{1,12},{2,15},{3,14},{4,9},{5,8},{6,11},{7,10},{8,5},{9,4},... | collective-permute-start | bytes 589832 | tf_op jit(solution)/shard_map/ppermute | solution.py:313
  204.0 5.4 %collective-permute-start.14 = (f32[2,16,1536]{2,1,0:T(8,128)}, f32[2,16,1536]{2,1,0:T(8,128)S(1)}, u32[]{:S(2)}, u32[]{:S(2)}) collective-permute-start(f32[2,16,1536]{2,1,0:T(8,128)} %get-tuple-element.56), channel_id=1, source_target_pairs={{0,15},{1,14},{2,13},{3,12},{4,11},{5,10},{6,9},{7,8},{8,7},{9,6},... | collective-permute-start | bytes 589832 | tf_op jit(solution)/shard_map/ppermute | solution.py:313
  209.5 1.6 collective-permute-start.2
  212.5 2.4 collective-permute-done.13.refs_15_
  214.9 2.0 collective-permute-start.5
  216.8 2.2 collective-permute-done.14.refs_16_
  220.2 1.5 collective-permute-done.2.refs_4_
  221.7 3.0 collective-permute-start.7
  224.7 6.5 %collective-permute-done.3.refs_5_ = f32[2,16,1536]{2,1,0:T(8,128)S(1)} collective-permute-done((f32[2,16,1536]{2,1,0:T(8,128)}, f32[2,16,1536]{2,1,0:T(8,128)S(1)}, u32[]{:S(2)}, u32[]{:S(2)}) %collective-permute-start.3) | collective-permute-done | bytes 196640 | tf_op jit(solution)/shard_map/ppermute | solution.py:313
  231.1 1.5 collective-permute-start.8
  232.7 2.5 collective-permute-done.4.refs_6_
  235.2 4.2 %collective-permute-start.9 = (f32[2,16,1536]{2,1,0:T(8,128)}, f32[2,16,1536]{2,1,0:T(8,128)S(1)}, u32[]{:S(2)}, u32[]{:S(2)}) collective-permute-start(f32[2,16,1536]{2,1,0:T(8,128)} %get-tuple-element.51), channel_id=1, source_target_pairs={{0,10},{1,11},{2,8},{3,9},{4,14},{5,15},{6,12},{7,13},{8,2},{9,3},... | collective-permute-start | bytes 589832 | tf_op jit(solution)/shard_map/ppermute | solution.py:313
  239.4 5.4 %collective-permute-done.9.refs_11_ = f32[2,16,1536]{2,1,0:T(8,128)S(1)} collective-permute-done((f32[2,16,1536]{2,1,0:T(8,128)}, f32[2,16,1536]{2,1,0:T(8,128)S(1)}, u32[]{:S(2)}, u32[]{:S(2)}) %collective-permute-start.9) | collective-permute-done | bytes 196640 | tf_op jit(solution)/shard_map/ppermute | solution.py:313
  245.5 24.2 %density_early.1 = (f32[512,1536]{1,0:T(8,128)}, bf16[1024,2048]{1,0:T(8,128)(2,1)}) custom-call(f32[2,512,512]{2,1,0:T(8,128)} %refs_0_.1, f32[2,16,1536]{2,1,0:T(8,128)} %get-tuple-element.41.refs_1_, f32[2,16,1536]{2,1,0:T(8,128)} %copy-done.8, f32[2,16,1536]{2,1,0:T(8,128)} %copy-done.9, f32[2,16,1536]{2,1,0:T(8,128)} %copy-done.18, ...), custom_call_target="tpu_custom_call" | custom-call | flops 15300820992 | bytes 16777216 | tf_op jit(solution)/shard_map/density_early/pallas_call | solution.py:251
  269.7 8.6 %density_late.1 = (f32[4,4,16,1024]{3,2,1,0:T(8,128)S(1)}, f32[4,4,16,1024]{3,2,1,0:T(8,128)S(1)}) custom-call(bf16[1024,2048]{1,0:T(8,128)(2,1)} %get-tuple-element.73.matrix_far, f32[32,2,16,512]{3,2,1,0:T(8,128)S(1)} %all-to-all-done.parts, f32[512,1536]{1,0:T(8,128)} %get-tuple-element.74.sums_far), custom_call_target="tpu_custom_call" | custom-call | flops 5100273664 | bytes 16777216 | tf_op jit(solution)/shard_map/density_late/pallas_call | solution.py:278
  278.4 2.6 collective-permute-done.31
  283.3 1.5 collective-permute-start.34
  284.7 6.6 %collective-permute-done.32 = f32[4,16,1024]{2,1,0:T(8,128)S(1)} collective-permute-done((f32[4,16,1024]{2,1,0:T(8,128)S(1)}, f32[4,16,1024]{2,1,0:T(8,128)S(1)}, u32[]{:S(2)}, u32[]{:S(2)}) %collective-permute-start.32) | collective-permute-done | bytes 262176 | tf_op jit(solution)/shard_map/ppermute | solution.py:322
  291.4 4.7 %collective-permute-done.33 = f32[4,16,1024]{2,1,0:T(8,128)S(1)} collective-permute-done((f32[4,16,1024]{2,1,0:T(8,128)S(1)}, f32[4,16,1024]{2,1,0:T(8,128)S(1)}, u32[]{:S(2)}, u32[]{:S(2)}) %collective-permute-start.33) | collective-permute-done | bytes 262176 | tf_op jit(solution)/shard_map/ppermute | solution.py:322
  296.2 2.0 collective-permute-start.35
  298.2 1.6 collective-permute-start.36
  300.6 1.7 collective-permute-done.35
  302.3 3.6 %collective-permute-done.36 = f32[16,1024]{1,0:T(8,128)S(1)} collective-permute-done((f32[16,1024]{1,0:T(8,128)S(1)}, f32[16,1024]{1,0:T(8,128)S(1)}, u32[]{:S(2)}, u32[]{:S(2)}) %collective-permute-start.36) | collective-permute-done | bytes 65568 | tf_op jit(solution)/shard_map/ppermute | solution.py:322
  (96 shorter events, 12.8 us)
Async XLA Ops:
  8.1 261.6 %all-to-all-start = ((f32[32,2,16,512]{3,2,1,0:T(8,128)}), f32[32,2,16,512]{3,2,1,0:T(8,128)S(1)}, u32[]{:S(2)}, u32[]{:S(2)}) async-start(f32[32,2,16,512]{3,2,1,0:T(8,128)} %shard_map.68), calls=%async_computation | async-start | bytes 4194304 | tf_op jit(solution)/shard_map/all_to_all | solution.py:315
  21.5 68.6 %collective-permute-start.15 = (f32[2,16,1536]{2,1,0:T(8,128)}, f32[2,16,1536]{2,1,0:T(8,128)S(1)}, u32[]{:S(2)}, u32[]{:S(2)}) collective-permute-start(f32[2,16,1536]{2,1,0:T(8,128)} %get-tuple-element.57), channel_id=1, source_target_pairs={{0,16},{1,17},{2,18},{3,19},{4,20},{5,21},{6,22},{7,23},{8,24},{9,... | collective-permute-start | bytes 589832 | tf_op jit(solution)/shard_map/ppermute | solution.py:313
  24.0 73.4 %collective-permute-start.16 = (f32[2,16,1536]{2,1,0:T(8,128)}, f32[2,16,1536]{2,1,0:T(8,128)S(1)}, u32[]{:S(2)}, u32[]{:S(2)}) collective-permute-start(f32[2,16,1536]{2,1,0:T(8,128)} %get-tuple-element.58), channel_id=1, source_target_pairs={{0,17},{1,16},{2,19},{3,18},{4,21},{5,20},{6,23},{7,22},{8,25},{9,... | collective-permute-start | bytes 589832 | tf_op jit(solution)/shard_map/ppermute | solution.py:313
  24.0 88.0 %collective-permute-start.17 = (f32[2,16,1536]{2,1,0:T(8,128)}, f32[2,16,1536]{2,1,0:T(8,128)S(1)}, u32[]{:S(2)}, u32[]{:S(2)}) collective-permute-start(f32[2,16,1536]{2,1,0:T(8,128)} %get-tuple-element.59), channel_id=1, source_target_pairs={{0,18},{1,19},{2,16},{3,17},{4,22},{5,23},{6,20},{7,21},{8,26},{9,... | collective-permute-start | bytes 589832 | tf_op jit(solution)/shard_map/ppermute | solution.py:313
  27.3 87.8 %collective-permute-start.18 = (f32[2,16,1536]{2,1,0:T(8,128)}, f32[2,16,1536]{2,1,0:T(8,128)S(1)}, u32[]{:S(2)}, u32[]{:S(2)}) collective-permute-start(f32[2,16,1536]{2,1,0:T(8,128)} %get-tuple-element.60), channel_id=1, source_target_pairs={{0,19},{1,18},{2,17},{3,16},{4,23},{5,22},{6,21},{7,20},{8,27},{9,... | collective-permute-start | bytes 589832 | tf_op jit(solution)/shard_map/ppermute | solution.py:313
  27.7 92.7 %collective-permute-start.19 = (f32[2,16,1536]{2,1,0:T(8,128)}, f32[2,16,1536]{2,1,0:T(8,128)S(1)}, u32[]{:S(2)}, u32[]{:S(2)}) collective-permute-start(f32[2,16,1536]{2,1,0:T(8,128)} %get-tuple-element.61), channel_id=1, source_target_pairs={{0,20},{1,21},{2,22},{3,23},{4,16},{5,17},{6,18},{7,19},{8,28},{9,... | collective-permute-start | bytes 589832 | tf_op jit(solution)/shard_map/ppermute | solution.py:313
  90.1 41.7 %collective-permute-start.20 = (f32[2,16,1536]{2,1,0:T(8,128)}, f32[2,16,1536]{2,1,0:T(8,128)S(1)}, u32[]{:S(2)}, u32[]{:S(2)}) collective-permute-start(f32[2,16,1536]{2,1,0:T(8,128)} %get-tuple-element.62), channel_id=1, source_target_pairs={{0,21},{1,20},{2,23},{3,22},{4,17},{5,16},{6,19},{7,18},{8,29},{9,... | collective-permute-start | bytes 589832 | tf_op jit(solution)/shard_map/ppermute | solution.py:313
  97.4 68.0 %copy-start.1 = (f32[2,16,1536]{2,1,0:T(8,128)}, f32[2,16,1536]{2,1,0:T(8,128)S(1)}, u32[]{:S(2)}) copy-start(f32[2,16,1536]{2,1,0:T(8,128)S(1)} %collective-permute-done.16.refs_18_) | copy-start | bytes 589828
  97.4 40.8 %collective-permute-start.21 = (f32[2,16,1536]{2,1,0:T(8,128)}, f32[2,16,1536]{2,1,0:T(8,128)S(1)}, u32[]{:S(2)}, u32[]{:S(2)}) collective-permute-start(f32[2,16,1536]{2,1,0:T(8,128)} %get-tuple-element.63), channel_id=1, source_target_pairs={{0,22},{1,23},{2,20},{3,21},{4,18},{5,19},{6,16},{7,17},{8,30},{9,... | collective-permute-start | bytes 589832 | tf_op jit(solution)/shard_map/ppermute | solution.py:313
  112.0 53.4 %copy-start.2 = (f32[2,16,1536]{2,1,0:T(8,128)}, f32[2,16,1536]{2,1,0:T(8,128)S(1)}, u32[]{:S(2)}) copy-start(f32[2,16,1536]{2,1,0:T(8,128)S(1)} %collective-permute-done.17.refs_19_) | copy-start | bytes 589828
  112.0 37.7 %collective-permute-start.22 = (f32[2,16,1536]{2,1,0:T(8,128)}, f32[2,16,1536]{2,1,0:T(8,128)S(1)}, u32[]{:S(2)}, u32[]{:S(2)}) collective-permute-start(f32[2,16,1536]{2,1,0:T(8,128)} %get-tuple-element.64), channel_id=1, source_target_pairs={{0,23},{1,22},{2,21},{3,20},{4,19},{5,18},{6,17},{7,16},{8,31},{9,... | collective-permute-start | bytes 589832 | tf_op jit(solution)/shard_map/ppermute | solution.py:313
  115.1 50.3 %copy-start.3 = (f32[2,16,1536]{2,1,0:T(8,128)}, f32[2,16,1536]{2,1,0:T(8,128)S(1)}, u32[]{:S(2)}) copy-start(f32[2,16,1536]{2,1,0:T(8,128)S(1)} %collective-permute-done.18.refs_20_) | copy-start | bytes 589828
  115.1 36.0 %collective-permute-start.23 = (f32[2,16,1536]{2,1,0:T(8,128)}, f32[2,16,1536]{2,1,0:T(8,128)}, u32[]{:S(2)}, u32[]{:S(2)}) collective-permute-start(f32[2,16,1536]{2,1,0:T(8,128)} %get-tuple-element.65), channel_id=1, source_target_pairs={{0,24},{1,25},{2,26},{3,27},{4,28},{5,29},{6,30},{7,31},{8,16},{9,... | collective-permute-start | bytes 589832 | tf_op jit(solution)/shard_map/ppermute | solution.py:313
  120.4 45.1 %copy-start.4 = (f32[2,16,1536]{2,1,0:T(8,128)}, f32[2,16,1536]{2,1,0:T(8,128)S(1)}, u32[]{:S(2)}) copy-start(f32[2,16,1536]{2,1,0:T(8,128)S(1)} %collective-permute-done.19.refs_21_) | copy-start | bytes 589828
  120.4 34.4 %collective-permute-start.24 = (f32[2,16,1536]{2,1,0:T(8,128)}, f32[2,16,1536]{2,1,0:T(8,128)}, u32[]{:S(2)}, u32[]{:S(2)}) collective-permute-start(f32[2,16,1536]{2,1,0:T(8,128)} %get-tuple-element.66), channel_id=1, source_target_pairs={{0,25},{1,24},{2,27},{3,26},{4,29},{5,28},{6,31},{7,30},{8,17},{9,... | collective-permute-start | bytes 589832 | tf_op jit(solution)/shard_map/ppermute | solution.py:313
  131.9 25.9 %collective-permute-start.25 = (f32[2,16,1536]{2,1,0:T(8,128)}, f32[2,16,1536]{2,1,0:T(8,128)}, u32[]{:S(2)}, u32[]{:S(2)}) collective-permute-start(f32[2,16,1536]{2,1,0:T(8,128)} %get-tuple-element.67), channel_id=1, source_target_pairs={{0,26},{1,27},{2,24},{3,25},{4,30},{5,31},{6,28},{7,29},{8,18},{9,... | collective-permute-start | bytes 589832 | tf_op jit(solution)/shard_map/ppermute | solution.py:313
  138.2 32.7 %collective-permute-start.26 = (f32[2,16,1536]{2,1,0:T(8,128)}, f32[2,16,1536]{2,1,0:T(8,128)}, u32[]{:S(2)}, u32[]{:S(2)}) collective-permute-start(f32[2,16,1536]{2,1,0:T(8,128)} %get-tuple-element.68), channel_id=1, source_target_pairs={{0,27},{1,26},{2,25},{3,24},{4,31},{5,30},{6,29},{7,28},{8,19},{9,... | collective-permute-start | bytes 589832 | tf_op jit(solution)/shard_map/ppermute | solution.py:313
  149.7 22.2 %collective-permute-start.27 = (f32[2,16,1536]{2,1,0:T(8,128)}, f32[2,16,1536]{2,1,0:T(8,128)}, u32[]{:S(2)}, u32[]{:S(2)}) collective-permute-start(f32[2,16,1536]{2,1,0:T(8,128)} %get-tuple-element.69), channel_id=1, source_target_pairs={{0,28},{1,29},{2,30},{3,31},{4,24},{5,25},{6,26},{7,27},{8,20},{9,... | collective-permute-start | bytes 589832 | tf_op jit(solution)/shard_map/ppermute | solution.py:313
  151.2 21.4 %collective-permute-start.28 = (f32[2,16,1536]{2,1,0:T(8,128)}, f32[2,16,1536]{2,1,0:T(8,128)}, u32[]{:S(2)}, u32[]{:S(2)}) collective-permute-start(f32[2,16,1536]{2,1,0:T(8,128)} %get-tuple-element.70), channel_id=1, source_target_pairs={{0,29},{1,28},{2,31},{3,30},{4,25},{5,24},{6,27},{7,26},{8,21},{9,... | collective-permute-start | bytes 589832 | tf_op jit(solution)/shard_map/ppermute | solution.py:313
  154.7 39.0 %collective-permute-start.29 = (f32[2,16,1536]{2,1,0:T(8,128)}, f32[2,16,1536]{2,1,0:T(8,128)}, u32[]{:S(2)}, u32[]{:S(2)}) collective-permute-start(f32[2,16,1536]{2,1,0:T(8,128)} %get-tuple-element.71), channel_id=1, source_target_pairs={{0,30},{1,31},{2,28},{3,29},{4,26},{5,27},{6,24},{7,25},{8,22},{9,... | collective-permute-start | bytes 589832 | tf_op jit(solution)/shard_map/ppermute | solution.py:313
  157.8 40.2 %collective-permute-start.30 = (f32[2,16,1536]{2,1,0:T(8,128)}, f32[2,16,1536]{2,1,0:T(8,128)}, u32[]{:S(2)}, u32[]{:S(2)}) collective-permute-start(f32[2,16,1536]{2,1,0:T(8,128)} %get-tuple-element.72), channel_id=1, source_target_pairs={{0,31},{1,30},{2,29},{3,28},{4,27},{5,26},{6,25},{7,24},{8,23},{9,... | collective-permute-start | bytes 589832 | tf_op jit(solution)/shard_map/ppermute | solution.py:313
  165.5 46.1 %copy-start.14 = (f32[2,16,1536]{2,1,0:T(8,128)S(1)}, f32[2,16,1536]{2,1,0:T(8,128)}, u32[]{:S(2)}) copy-start(f32[2,16,1536]{2,1,0:T(8,128)} %get-tuple-element.46) | copy-start | bytes 589828
  165.5 49.4 %copy-start.12 = (f32[2,16,1536]{2,1,0:T(8,128)S(1)}, f32[2,16,1536]{2,1,0:T(8,128)}, u32[]{:S(2)}) copy-start(f32[2,16,1536]{2,1,0:T(8,128)} %get-tuple-element.47) | copy-start | bytes 589828
  165.5 53.6 %copy-start.11 = (f32[2,16,1536]{2,1,0:T(8,128)S(1)}, f32[2,16,1536]{2,1,0:T(8,128)}, u32[]{:S(2)}) copy-start(f32[2,16,1536]{2,1,0:T(8,128)} %get-tuple-element.48) | copy-start | bytes 589828
  170.9 32.0 %collective-permute-start = (f32[2,16,1536]{2,1,0:T(8,128)}, f32[2,16,1536]{2,1,0:T(8,128)S(1)}, u32[]{:S(2)}, u32[]{:S(2)}) collective-permute-start(f32[2,16,1536]{2,1,0:T(8,128)} %get-tuple-element.42), channel_id=1, source_target_pairs={{0,1},{1,0},{2,3},{3,2},{4,5},{5,4},{6,7},{7,6},{8,9},{9,8},{10,11... | collective-permute-start | bytes 589832 | tf_op jit(solution)/shard_map/ppermute | solution.py:313
  172.0 32.1 %collective-permute-start.1 = (f32[2,16,1536]{2,1,0:T(8,128)}, f32[2,16,1536]{2,1,0:T(8,128)S(1)}, u32[]{:S(2)}, u32[]{:S(2)}) collective-permute-start(f32[2,16,1536]{2,1,0:T(8,128)} %get-tuple-element.43), channel_id=1, source_target_pairs={{0,2},{1,3},{2,0},{3,1},{4,6},{5,7},{6,4},{7,5},{8,10},{9,11},{10,... | collective-permute-start | bytes 589832 | tf_op jit(solution)/shard_map/ppermute | solution.py:313
  172.5 36.9 %collective-permute-start.10 = (f32[2,16,1536]{2,1,0:T(8,128)}, f32[2,16,1536]{2,1,0:T(8,128)S(1)}, u32[]{:S(2)}, u32[]{:S(2)}) collective-permute-start(f32[2,16,1536]{2,1,0:T(8,128)} %get-tuple-element.52), channel_id=1, source_target_pairs={{0,11},{1,10},{2,9},{3,8},{4,15},{5,14},{6,13},{7,12},{8,3},{9,2},... | collective-permute-start | bytes 589832 | tf_op jit(solution)/shard_map/ppermute | solution.py:313
  193.8 17.3 %collective-permute-start.11 = (f32[2,16,1536]{2,1,0:T(8,128)}, f32[2,16,1536]{2,1,0:T(8,128)S(1)}, u32[]{:S(2)}, u32[]{:S(2)}) collective-permute-start(f32[2,16,1536]{2,1,0:T(8,128)} %get-tuple-element.53), channel_id=1, source_target_pairs={{0,12},{1,13},{2,14},{3,15},{4,8},{5,9},{6,10},{7,11},{8,4},{9,5},... | collective-permute-start | bytes 589832 | tf_op jit(solution)/shard_map/ppermute | solution.py:313
  198.0 13.6 %collective-permute-start.12 = (f32[2,16,1536]{2,1,0:T(8,128)}, f32[2,16,1536]{2,1,0:T(8,128)S(1)}, u32[]{:S(2)}, u32[]{:S(2)}) collective-permute-start(f32[2,16,1536]{2,1,0:T(8,128)} %get-tuple-element.54), channel_id=1, source_target_pairs={{0,13},{1,12},{2,15},{3,14},{4,9},{5,8},{6,11},{7,10},{8,5},{9,4},... | collective-permute-start | bytes 589832 | tf_op jit(solution)/shard_map/ppermute | solution.py:313
  203.0 41.9 %copy-start.8 = (f32[2,16,1536]{2,1,0:T(8,128)}, f32[2,16,1536]{2,1,0:T(8,128)S(1)}, u32[]{:S(2)}) copy-start(f32[2,16,1536]{2,1,0:T(8,128)S(1)} %collective-permute-done.refs_2_) | copy-start | bytes 589828
  203.0 11.9 %collective-permute-start.13 = (f32[2,16,1536]{2,1,0:T(8,128)}, f32[2,16,1536]{2,1,0:T(8,128)S(1)}, u32[]{:S(2)}, u32[]{:S(2)}) collective-permute-start(f32[2,16,1536]{2,1,0:T(8,128)} %get-tuple-element.55), channel_id=1, source_target_pairs={{0,14},{1,15},{2,12},{3,13},{4,10},{5,11},{6,8},{7,9},{8,6},{9,7},... | collective-permute-start | bytes 589832 | tf_op jit(solution)/shard_map/ppermute | solution.py:313
  204.0 40.8 %copy-start.9 = (f32[2,16,1536]{2,1,0:T(8,128)}, f32[2,16,1536]{2,1,0:T(8,128)S(1)}, u32[]{:S(2)}) copy-start(f32[2,16,1536]{2,1,0:T(8,128)S(1)} %collective-permute-done.1.refs_3_) | copy-start | bytes 589828
  204.0 15.0 %collective-permute-start.14 = (f32[2,16,1536]{2,1,0:T(8,128)}, f32[2,16,1536]{2,1,0:T(8,128)S(1)}, u32[]{:S(2)}, u32[]{:S(2)}) collective-permute-start(f32[2,16,1536]{2,1,0:T(8,128)} %get-tuple-element.56), channel_id=1, source_target_pairs={{0,15},{1,14},{2,13},{3,12},{4,11},{5,10},{6,9},{7,8},{8,7},{9,6},... | collective-permute-start | bytes 589832 | tf_op jit(solution)/shard_map/ppermute | solution.py:313
  209.5 12.2 %collective-permute-start.2 = (f32[2,16,1536]{2,1,0:T(8,128)}, f32[2,16,1536]{2,1,0:T(8,128)S(1)}, u32[]{:S(2)}, u32[]{:S(2)}) collective-permute-start(f32[2,16,1536]{2,1,0:T(8,128)} %get-tuple-element.44), channel_id=1, source_target_pairs={{0,3},{1,2},{2,1},{3,0},{4,7},{5,6},{6,5},{7,4},{8,11},{9,10},{10,... | collective-permute-start | bytes 589832 | tf_op jit(solution)/shard_map/ppermute | solution.py:313
  211.0 20.1 %collective-permute-start.3 = (f32[2,16,1536]{2,1,0:T(8,128)}, f32[2,16,1536]{2,1,0:T(8,128)S(1)}, u32[]{:S(2)}, u32[]{:S(2)}) collective-permute-start(f32[2,16,1536]{2,1,0:T(8,128)} %get-tuple-element.45), channel_id=1, source_target_pairs={{0,4},{1,5},{2,6},{3,7},{4,0},{5,1},{6,2},{7,3},{8,12},{9,13},{10,... | collective-permute-start | bytes 589832 | tf_op jit(solution)/shard_map/ppermute | solution.py:313
  211.6 23.5 %collective-permute-start.4 = (f32[2,16,1536]{2,1,0:T(8,128)S(1)}, f32[2,16,1536]{2,1,0:T(8,128)S(1)}, u32[]{:S(2)}, u32[]{:S(2)}) collective-permute-start(f32[2,16,1536]{2,1,0:T(8,128)S(1)} %copy-done.14), channel_id=1, source_target_pairs={{0,5},{1,4},{2,7},{3,6},{4,1},{5,0},{6,3},{7,2},{8,13},{9,12},{10,... | collective-permute-start | bytes 589832 | tf_op jit(solution)/shard_map/ppermute | solution.py:313
  214.9 24.5 %collective-permute-start.5 = (f32[2,16,1536]{2,1,0:T(8,128)S(1)}, f32[2,16,1536]{2,1,0:T(8,128)S(1)}, u32[]{:S(2)}, u32[]{:S(2)}) collective-permute-start(f32[2,16,1536]{2,1,0:T(8,128)S(1)} %copy-done.12), channel_id=1, source_target_pairs={{0,6},{1,7},{2,4},{3,5},{4,2},{5,3},{6,0},{7,1},{8,14},{9,15},{10,... | collective-permute-start | bytes 589832 | tf_op jit(solution)/shard_map/ppermute | solution.py:313
  219.1 20.3 %collective-permute-start.6 = (f32[2,16,1536]{2,1,0:T(8,128)S(1)}, f32[2,16,1536]{2,1,0:T(8,128)S(1)}, u32[]{:S(2)}, u32[]{:S(2)}) collective-permute-start(f32[2,16,1536]{2,1,0:T(8,128)S(1)} %copy-done.11), channel_id=1, source_target_pairs={{0,7},{1,6},{2,5},{3,4},{4,3},{5,2},{6,1},{7,0},{8,15},{9,14},{10,... | collective-permute-start | bytes 589832 | tf_op jit(solution)/shard_map/ppermute | solution.py:313
  221.7 17.7 %collective-permute-start.7 = (f32[2,16,1536]{2,1,0:T(8,128)}, f32[2,16,1536]{2,1,0:T(8,128)S(1)}, u32[]{:S(2)}, u32[]{:S(2)}) collective-permute-start(f32[2,16,1536]{2,1,0:T(8,128)} %get-tuple-element.49), channel_id=1, source_target_pairs={{0,8},{1,9},{2,10},{3,11},{4,12},{5,13},{6,14},{7,15},{8,0},{9,1},... | collective-permute-start | bytes 589832 | tf_op jit(solution)/shard_map/ppermute | solution.py:313
  231.1 8.3 %collective-permute-start.8 = (f32[2,16,1536]{2,1,0:T(8,128)}, f32[2,16,1536]{2,1,0:T(8,128)S(1)}, u32[]{:S(2)}, u32[]{:S(2)}) collective-permute-start(f32[2,16,1536]{2,1,0:T(8,128)} %get-tuple-element.50), channel_id=1, source_target_pairs={{0,9},{1,8},{2,11},{3,10},{4,13},{5,12},{6,15},{7,14},{8,1},{9,0},... | collective-permute-start | bytes 589832 | tf_op jit(solution)/shard_map/ppermute | solution.py:313
  235.2 9.6 %collective-permute-start.9 = (f32[2,16,1536]{2,1,0:T(8,128)}, f32[2,16,1536]{2,1,0:T(8,128)S(1)}, u32[]{:S(2)}, u32[]{:S(2)}) collective-permute-start(f32[2,16,1536]{2,1,0:T(8,128)} %get-tuple-element.51), channel_id=1, source_target_pairs={{0,10},{1,11},{2,8},{3,9},{4,14},{5,15},{6,12},{7,13},{8,2},{9,3},... | collective-permute-start | bytes 589832 | tf_op jit(solution)/shard_map/ppermute | solution.py:313
  278.3 2.7 collective-permute-start.31
  281.2 10.2 %collective-permute-start.32 = (f32[4,16,1024]{2,1,0:T(8,128)S(1)}, f32[4,16,1024]{2,1,0:T(8,128)S(1)}, u32[]{:S(2)}, u32[]{:S(2)}) collective-permute-start(f32[4,16,1024]{2,1,0:T(8,128)S(1)} %get-tuple-element.80), channel_id=1, source_target_pairs={{0,6},{1,7},{2,4},{3,5},{4,2},{5,3},{6,0},{7,1},{8,14},{9,15},{10,... | collective-permute-start | bytes 786440 | tf_op jit(solution)/shard_map/ppermute | solution.py:322
  282.5 13.6 %collective-permute-start.33 = (f32[4,16,1024]{2,1,0:T(8,128)S(1)}, f32[4,16,1024]{2,1,0:T(8,128)S(1)}, u32[]{:S(2)}, u32[]{:S(2)}) collective-permute-start(f32[4,16,1024]{2,1,0:T(8,128)S(1)} %get-tuple-element.79), channel_id=1, source_target_pairs={{0,4},{1,5},{2,6},{3,7},{4,0},{5,1},{6,2},{7,3},{8,12},{9,13},{10,... | collective-permute-start | bytes 786440 | tf_op jit(solution)/shard_map/ppermute | solution.py:322
  283.3 12.8 %collective-permute-start.34 = (f32[4,16,1024]{2,1,0:T(8,128)S(1)}, f32[4,16,1024]{2,1,0:T(8,128)S(1)}, u32[]{:S(2)}, u32[]{:S(2)}) collective-permute-start(f32[4,16,1024]{2,1,0:T(8,128)S(1)} %get-tuple-element.78), channel_id=1, source_target_pairs={{0,2},{1,3},{2,0},{3,1},{4,6},{5,7},{6,4},{7,5},{8,10},{9,11},{10,... | collective-permute-start | bytes 786440 | tf_op jit(solution)/shard_map/ppermute | solution.py:322
  296.2 6.2 %collective-permute-start.35 = (f32[16,1024]{1,0:T(8,128)S(1)}, f32[16,1024]{1,0:T(8,128)S(1)}, u32[]{:S(2)}, u32[]{:S(2)}) collective-permute-start(f32[16,1024]{1,0:T(8,128)S(1)} %get-tuple-element.81), channel_id=1, source_target_pairs={{0,24},{1,25},{2,26},{3,27},{4,28},{5,29},{6,30},{7,31},{8,16},{9,... | collective-permute-start | bytes 196616 | tf_op jit(solution)/shard_map/ppermute | solution.py:322
  298.2 7.8 %collective-permute-start.36 = (f32[16,1024]{1,0:T(8,128)S(1)}, f32[16,1024]{1,0:T(8,128)S(1)}, u32[]{:S(2)}, u32[]{:S(2)}) collective-permute-start(f32[16,1024]{1,0:T(8,128)S(1)} %get-tuple-element.83), channel_id=1, source_target_pairs={{0,16},{1,17},{2,18},{3,19},{4,20},{5,21},{6,22},{7,23},{8,24},{9,... | collective-permute-start | bytes 196616 | tf_op jit(solution)/shard_map/ppermute | solution.py:322
  299.8 6.2 %collective-permute-start.37 = (f32[16,1024]{1,0:T(8,128)S(1)}, f32[16,1024]{1,0:T(8,128)S(1)}, u32[]{:S(2)}, u32[]{:S(2)}) collective-permute-start(f32[16,1024]{1,0:T(8,128)S(1)} %get-tuple-element.82), channel_id=1, source_target_pairs={{0,8},{1,9},{2,10},{3,11},{4,12},{5,13},{6,14},{7,15},{8,0},{9,1},... | collective-permute-start | bytes 196616 | tf_op jit(solution)/shard_map/ppermute | solution.py:322
  (17 other events, 292.5 us)
